TPU v7x, 32 devices: a whole 2x2x4 slice. The times are simulated.
32 devices in a mesh: cfg: 2 (over x), ta: 16 (over z, y, core).
Axes of the slice: x: 2, y: 2, z: 4, core: 2. Of those that a mesh axis runs over, the one named last changes fastest.
Arguments:
- fine_source: bfloat16 [32, 128, 2, 2, 24, 128], P('cfg', 'ta'), parts along dimension 0, may hold values from -24 to 24
- projectors: bfloat16 [32, 128, 2304], P(('cfg', 'ta')), parts along dimension 0, may hold values from -0.21875 to 0.21875
- stencil_links: bfloat16 [32, 8, 48, 864], P(('cfg', 'ta')), parts along dimension 0, may hold values from -0.21875 to 0.21875
- quark_mass: float32 [2], P('cfg'), parts along dimension 0, may hold values from 1.5 to 3
Outputs:
- solution: float32 [32, 8, 96, 128], P(('cfg', 'ta')), parts along dimension 0
- residual: float32 [32, 8, 96, 128], P(('cfg', 'ta')), parts along dimension 0
There are 2 independent parts, one for each index of `cfg`. A program takes and returns all parts, laid end to end along the dimension named above; each array names one. Nothing has to cross between parts.
All inputs are finite; a program needn't handle non-finite values.
Results may differ from a plain program's by a relative error of at most 0.012.
The roundings to bfloat16 on the way count: a program that leaves them out, or rounds other values in their place, can miss the bound.
Values may be sent and summed in bfloat16 or wider, within the bound.
A program may use at most 128 MiB of HBM per device.

v0:
```python
import functools
import math

import jax
import jax.numpy as jnp
from jax import lax
from jax.experimental import pallas as pl
from jax.experimental.pallas import tpu as pltpu
from jax.sharding import PartitionSpec as P

LX = 4
LZ = 8
ITERS = 3


def from_behind(value, axis, steps):
    count = lax.axis_size(axis)
    pairs = [(source, (source + steps) % count) for source in range(count)]
    return lax.ppermute(value, axis, pairs)


def real_weights(proj_view):
    proj_re = proj_view[..., 0, :]
    proj_im = proj_view[..., 1, :]
    first_row = jnp.stack([proj_re, proj_im], axis=-4)
    second_row = jnp.stack([-proj_im, proj_re], axis=-4)
    return jnp.stack([first_row, second_row], axis=-5)


def inner_local(left, right, comp_count):
    left_re = left[:, :comp_count]
    left_im = left[:, comp_count:]
    right_re = right[:, :comp_count]
    right_im = right[:, comp_count:]
    return (
        jnp.sum(left_re * right_re + left_im * right_im, axis=(0, 1)),
        jnp.sum(left_re * right_im - left_im * right_re, axis=(0, 1)),
    )


def scaled(vector, factor_re, factor_im, comp_count):
    vector_re = vector[:, :comp_count]
    vector_im = vector[:, comp_count:]
    return jnp.concatenate(
        [
            factor_re * vector_re - factor_im * vector_im,
            factor_re * vector_im + factor_im * vector_re,
        ],
        axis=1,
    )


def shards_general(fine_source, projectors, stencil_links, quark_mass):
    comp_count = stencil_links.shape[2]
    null_count = comp_count // 2
    site_count = stencil_links.shape[1]
    column_count = projectors.shape[1]
    block_count = column_count // site_count
    fine_count = fine_source.shape[4]
    rhs_count = fine_source.shape[5]
    plane_count = fine_source.shape[0]
    moved_proj = lax.all_to_all(projectors, "ta", split_axis=1, concat_axis=0, tiled=True)
    local_columns = fine_source.shape[1]
    group_size = math.gcd(block_count, local_columns)
    groups = local_columns // group_size
    weights = real_weights(
        moved_proj.reshape(plane_count, groups, group_size, 2, null_count, 2, fine_count)
    )
    fine_local = fine_source.reshape(plane_count, groups, group_size, 2, 2, fine_count, rhs_count)
    partial_sums = jnp.einsum(
        "pmgdchvk,pmgchkr->pmdhvr", weights, fine_local, preferred_element_type=jnp.float32
    )
    partial_sums = partial_sums.reshape(plane_count, groups, 2 * comp_count, rhs_count)
    collected = lax.all_to_all(partial_sums, "ta", split_axis=0, concat_axis=1, tiled=True)
    source = jnp.sum(
        collected.reshape(site_count, block_count // group_size, 2 * comp_count, rhs_count), axis=1
    )
    link_view = stencil_links.reshape(site_count, comp_count, 9, 2, comp_count)
    link_re = link_view[:, :, :, 0, :]
    link_im = link_view[:, :, :, 1, :]
    upper_rows = jnp.stack([link_re, -link_im], axis=3)
    lower_rows = jnp.stack([link_im, link_re], axis=3)
    real_operator = jnp.stack([upper_rows, lower_rows], axis=1).reshape(
        site_count, 2 * comp_count, 18 * comp_count
    )
    mass_value = quark_mass[0]
    z_position = lax.axis_index("ta") % LZ
    line_count = site_count // LX

    def flatten_sites(shifted):
        return shifted.reshape(site_count, 2 * comp_count, rhs_count)

    solution = jnp.zeros_like(source)
    residual = source
    basis_q = []
    basis_p = []
    for iteration in range(ITERS):
        direction = residual
        rounded = residual.astype(jnp.bfloat16)
        plane_view = rounded.reshape(line_count, LX, 2 * comp_count, rhs_count)
        x_plus = flatten_sites(jnp.roll(plane_view, -1, axis=1))
        x_minus = flatten_sites(jnp.roll(plane_view, 1, axis=1))
        y_plus = flatten_sites(jnp.roll(plane_view, -1, axis=0))
        y_minus = flatten_sites(jnp.roll(plane_view, 1, axis=0))
        z_plus_near = from_behind(rounded, "ta", -1)
        z_minus_near = from_behind(rounded, "ta", 1)
        upper_pair = from_behind(jnp.stack([rounded, z_minus_near], axis=0), "ta", -LZ)
        lower_pair = from_behind(jnp.stack([rounded, z_plus_near], axis=0), "ta", LZ)
        t_plus = upper_pair[0]
        t_minus = lower_pair[0]
        z_plus = jnp.where(z_position == LZ - 1, lower_pair[1], z_plus_near)
        z_minus = jnp.where(z_position == 0, upper_pair[1], z_minus_near)
        stacked = jnp.stack(
            [rounded, x_plus, x_minus, y_plus, y_minus, z_plus, z_minus, t_plus, t_minus], axis=1
        )
        stacked = stacked.reshape(site_count, 18 * comp_count, rhs_count)
        product = jnp.einsum(
            "sij,sjr->sir", real_operator, stacked, preferred_element_type=jnp.float32
        )
        mapped = product + mass_value * rounded.astype(jnp.float32)
        square_loc = inner_local(mapped, mapped, comp_count)[0]
        cross_re, cross_im = inner_local(mapped, residual, comp_count)
        if iteration > 0:
            coef_pairs = [inner_local(earlier, mapped, comp_count) for earlier in basis_q]
            back_pairs = [inner_local(earlier, residual, comp_count) for earlier in basis_q]
            coef_re = jnp.stack([pair[0] for pair in coef_pairs])
            coef_im = jnp.stack([pair[1] for pair in coef_pairs])
            back_re = jnp.stack([pair[0] for pair in back_pairs])
            back_im = jnp.stack([pair[1] for pair in back_pairs])
        else:
            coef_re = jnp.zeros((1, rhs_count), jnp.float32)
            coef_im = jnp.zeros((1, rhs_count), jnp.float32)
            back_re = jnp.zeros((1, rhs_count), jnp.float32)
            back_im = jnp.zeros((1, rhs_count), jnp.float32)
        square_all, cross_re, cross_im, coef_re, coef_im, back_re, back_im = lax.psum(
            (square_loc, cross_re, cross_im, coef_re, coef_im, back_re, back_im), "ta"
        )
        squared = square_all
        proj_re = cross_re
        proj_im = cross_im
        for number in range(iteration):
            mapped = mapped - scaled(basis_q[number], coef_re[number], coef_im[number], comp_count)
            direction = direction - scaled(
                basis_p[number], coef_re[number], coef_im[number], comp_count
            )
            squared = squared - (
                coef_re[number] * coef_re[number] + coef_im[number] * coef_im[number]
            )
            proj_re = proj_re - (
                coef_re[number] * back_re[number] + coef_im[number] * back_im[number]
            )
            proj_im = proj_im - (
                coef_re[number] * back_im[number] - coef_im[number] * back_re[number]
            )
        factor = 1.0 / jnp.sqrt(squared + 1e-06)
        unit_q = mapped * factor
        unit_p = direction * factor
        alpha_re = proj_re * factor
        alpha_im = proj_im * factor
        solution = solution + scaled(unit_p, alpha_re, alpha_im, comp_count)
        residual = residual - scaled(unit_q, alpha_re, alpha_im, comp_count)
        basis_q.append(unit_q)
        basis_p.append(unit_p)
    return (
        solution.reshape(1, site_count, 2 * comp_count, rhs_count),
        residual.reshape(1, site_count, 2 * comp_count, rhs_count),
    )


MESH = pl.DeviceIdType.MESH


def flipped(number, mask, bits):
    total = 0
    for bit in range(bits):
        size = 1 << bit
        total = total + (((number // size) % 2 + (mask // size) % 2) % 2) * size
    return total


def swapped(value):
    return pltpu.roll(value, value.shape[-1] // 2, value.ndim - 1)


def lower_lanes(shape):
    return lax.broadcasted_iota(jnp.int32, shape, len(shape) - 1) < shape[-1] // 2


def turned(value):
    other = swapped(value)
    return jnp.where(lower_lanes(value.shape), -other, other)


def widened(rounded):
    return jnp.concatenate(
        [rounded, turned(rounded.astype(jnp.float32)).astype(jnp.bfloat16)], axis=0
    )


def times(factor, value):
    return factor[0] * value + factor[1] * turned(value)


def solve_kernel(
    count, sites, comps,
    mass_ref, proj_ref, fine_hbm, links_hbm,
    sol_ref, res_ref,
    fine_ref, links_ref, near_ref, zlinks_ref, tlinks_ref, fold_ref,
    weights_ref, weights_in, part_keep, part_out, part_in, sum_out, source_ref,
    wide_ref, round_ref, halo_ref, acc_ref, sol_half, res_half, basis_q, basis_p, stat_out, stat_in,
    local_sem, wsend, wrecv, psend, precv, ssend, srecv, hsend, hrecv, gsend, grecv,
):
    me = lax.axis_index("ta")
    bits = count.bit_length() - 1
    core = me % 2
    chip = me // 2
    partner = chip * 2 + 1 - core
    chips = count // 2
    turns = [(1 - 2 * ((me // (1 << bit)) % 2)) * (1 << bit) for bit in range(bits)]
    others = [me]
    for step in range(1, count):
        top = step.bit_length() - 1
        others.append(others[step - (1 << top)] + turns[top])
    null = comps // 2
    rows = fine_ref.shape[1]
    rhs = fine_ref.shape[2]

    fine_copy = pltpu.make_async_copy(fine_hbm, fine_ref, local_sem.at[0])
    fine_copy.start()
    links_copy = pltpu.make_async_copy(links_hbm, links_ref, local_sem.at[1])
    links_copy.start()

    barrier = pltpu.get_barrier_semaphore()

    for other in others[1:]:
        pl.semaphore_signal(barrier, inc=1, device_id={"ta": other}, device_id_type=MESH)
    pl.semaphore_wait(barrier, count - 1)

    def weights_copy(slot, other, origin):
        return pltpu.make_async_remote_copy(
            src_ref=weights_ref.at[slot], dst_ref=weights_in.at[origin],
            send_sem=wsend.at[slot], recv_sem=wrecv.at[origin],
            device_id={"ta": other}, device_id_type=MESH,
        )

    columns = proj_ref.shape[1]
    width = columns * comps
    groups = comps // columns
    lane_at = lax.broadcasted_iota(jnp.int32, (columns, width), 1) // comps
    row_at = lax.broadcasted_iota(jnp.int32, (columns, width), 0)
    picks = (lane_at == row_at).astype(jnp.float32)
    fold_row = lax.broadcasted_iota(jnp.int32, (width, width), 0) % comps
    fold_lane = lax.broadcasted_iota(jnp.int32, (width, width), 1) % comps
    fold_ref[...] = (fold_row == fold_lane).astype(jnp.float32).astype(jnp.bfloat16)

    def arrange(slot):
        raw = proj_ref[slot].astype(jnp.float32)
        pieces = []
        for column in range(columns):
            for group in range(groups):
                row = raw[column : column + 1, group * width : (group + 1) * width]
                pieces.append(row * picks)
        left = jnp.concatenate(pieces, axis=0).astype(jnp.bfloat16)
        spread = jnp.dot(left, fold_ref[...], preferred_element_type=jnp.float32)
        total = spread[:comps] * picks[0:1]
        for column in range(1, columns):
            block = spread[column * comps : (column + 1) * comps]
            total = total + block * picks[column : column + 1]
        weights_ref[slot] = total.astype(jnp.bfloat16)

    def send_weights(step, carry):
        other = flipped(me, count - 1 - step, bits)
        arrange(other)
        weights_copy(other, other, me).start()
        return carry

    lax.fori_loop(0, count - 1, send_weights, 0)
    arrange(me)

    links_copy.wait()
    for site in range(sites):
        near_ref[site] = links_ref[site, :, : 10 * comps]
        zlinks_ref[site] = links_ref[site, :, 10 * comps : 14 * comps]
        tlinks_ref[site] = links_ref[site, :, 14 * comps : 18 * comps]
    fine_copy.wait()

    def restricted(plane, weights):
        fine = fine_ref[plane].astype(jnp.float32).reshape(columns, 2, 2, null, rhs)

        def ordered(real, imag, half):
            view = jnp.stack([real[:, half], imag[:, half]], axis=1)
            return view.reshape(width, rhs).astype(jnp.bfloat16)

        real, imag = fine[:, 0], fine[:, 1]
        right = jnp.concatenate(
            [ordered(real, imag, 0), ordered(real, imag, 1),
             ordered(imag, -real, 0), ordered(imag, -real, 1)], axis=1
        )
        total = jnp.dot(weights, right, preferred_element_type=jnp.float32)
        real = jnp.concatenate([total[:null, :rhs], total[null:, rhs : 2 * rhs]], axis=0)
        imag = jnp.concatenate(
            [total[:null, 2 * rhs : 3 * rhs], total[null:, 3 * rhs :]], axis=0
        )
        low = lower_lanes(real.shape)
        return jnp.stack(
            [jnp.where(low, real, swapped(imag)), jnp.where(low, swapped(real), imag)], axis=0
        )

    def part_copy(slot):
        return pltpu.make_async_remote_copy(
            src_ref=part_out.at[slot], dst_ref=part_in.at[slot],
            send_sem=psend.at[slot], recv_sem=precv.at[slot],
            device_id={"ta": partner}, device_id_type=MESH,
        )

    def source_copy(slot, origin):
        return pltpu.make_async_remote_copy(
            src_ref=sum_out.at[slot], dst_ref=source_ref.at[origin],
            send_sem=ssend.at[slot], recv_sem=srecv.at[origin],
            device_id={"ta": flipped(chip, slot, bits - 1) * 2 + core}, device_id_type=MESH,
        )

    def pair(step):
        other = flipped(chip, step, bits - 1)
        away = other * 2 + 1 - core
        weights_copy(me, partner, away).wait_recv()
        part_out[step] = restricted(away, weights_in[away])
        part_copy(step).start()
        kept = other * 2 + core
        weights_copy(me, partner, kept).wait_recv()
        part_keep[step] = restricted(kept, weights_in[kept])

    def finish(step):
        part_copy(step).wait_recv()
        sum_out[step] = part_keep[step] + part_in[step]
        source_copy(step, chip).start()

    weights_copy(me, partner, partner).wait_recv()
    part_out[0] = restricted(partner, weights_in[partner])
    part_copy(0).start()
    part_keep[0] = restricted(me, weights_ref[me])
    pair(1)
    part_copy(0).wait_recv()
    source_ref[chip] = part_keep[0] + part_in[0]

    def pair_step(step, carry):
        pair(step)
        finish(step - 1)
        return carry

    lax.fori_loop(2, chips, pair_step, 0)
    finish(chips - 1)

    for step in range(1, chips):
        source_copy(step, others[2 * step] // 2).wait_recv()

    mass = mass_ref[0]
    base = (me // LZ) * LZ
    z_at = me % LZ
    above = base + (z_at + 1) % LZ
    below = base + (z_at + LZ - 1) % LZ
    other_time = (me + LZ) % count
    targets = (other_time, above, below)
    lines = sites // LX

    def place(site, dx, dy):
        return ((site // LX + dy) % lines) * LX + (site % LX + dx) % LX

    def halo_copy(it, half, which):
        return pltpu.make_async_remote_copy(
            src_ref=round_ref.at[it, half], dst_ref=halo_ref.at[it, half, which],
            send_sem=hsend.at[it, half, which], recv_sem=hrecv.at[it, half, which],
            device_id={"ta": targets[which]}, device_id_type=MESH,
        )

    def stat_copy(it, half, other, origin):
        return pltpu.make_async_remote_copy(
            src_ref=stat_out.at[it, half], dst_ref=stat_in.at[it, half, origin],
            send_sem=gsend.at[it, half, other], recv_sem=grecv.at[it, half, origin],
            device_id={"ta": other}, device_id_type=MESH,
        )

    def residual_at(it, half, site):
        return source_ref[site, half] if it == 0 else res_half[half, site]

    def send_halo(it, half):
        for site in range(sites):
            round_ref[it, half, site] = residual_at(it, half, site).astype(jnp.bfloat16)
        for which in range(3):
            halo_copy(it, half, which).start()

    def near_product(it, half):
        for site in range(sites):
            wide_ref[half, site] = widened(round_ref[it, half, site])
        steps = ((0, 0), (1, 0), (-1, 0), (0, 1), (0, -1))
        for site in range(sites):
            right = jnp.concatenate(
                [wide_ref[half, place(site, dx, dy)] for dx, dy in steps], axis=0
            )
            acc_ref[half, site] = jnp.dot(
                near_ref[site], right, preferred_element_type=jnp.float32
            )

    def far_product(it, half):
        halo_copy(it, half, 2).wait_recv()
        halo_copy(it, half, 1).wait_recv()
        for site in range(sites):
            right = jnp.concatenate(
                [widened(halo_ref[it, half, 2, site]), widened(halo_ref[it, half, 1, site])],
                axis=0,
            )
            acc_ref[half, site] += jnp.dot(
                zlinks_ref[site], right, preferred_element_type=jnp.float32
            )
        halo_copy(it, half, 0).wait_recv()
        sums = [0.0] * (3 + 2 * it)
        for site in range(sites):
            wide = widened(halo_ref[it, half, 0, site])
            right = jnp.concatenate([wide, wide], axis=0)
            product = acc_ref[half, site] + jnp.dot(
                tlinks_ref[site], right, preferred_element_type=jnp.float32
            )
            q = product + mass * round_ref[it, half, site].astype(jnp.float32)
            acc_ref[half, site] = q
            r = residual_at(it, half, site)
            q_other = swapped(q)
            sums[0] += q * q
            sums[1] += q * r
            sums[2] += q * swapped(r)
            for j in range(it):
                b = basis_q[j, half, site]
                sums[3 + 2 * j] += b * q
                sums[4 + 2 * j] += b * q_other
        lines_of = [jnp.sum(value, axis=0, keepdims=True) for value in sums]
        lines_of += [jnp.zeros((8 - len(lines_of), rhs), jnp.float32)]
        stats = jnp.concatenate(lines_of, axis=0)
        stat_out[it, half] = stats

        for other in others[:0:-1]:
            stat_copy(it, half, other, me).start()
        stat_in[it, half, me] = stats

    scalars = [([], [], [], []) for _ in range(2)]

    def update(it, half):
        for other in others[1:]:
            stat_copy(it, half, other, other).wait_recv()
        total = jnp.sum(stat_in[it, half], axis=0)
        moved = swapped(total)
        reals = total + moved
        imags = jnp.where(lower_lanes(total.shape), total - moved, moved - total)
        backs, epsilons, overlaps, _ = scalars[half]
        squared, cross_re, cross_im = reals[0:1], reals[1:2], imags[2:3]
        coefs = [
            (reals[3 + 2 * j : 4 + 2 * j], imags[4 + 2 * j : 5 + 2 * j]) for j in range(it)
        ]
        for j, (c_re, c_im) in enumerate(coefs):
            squared = squared - (c_re * c_re + c_im * c_im) * (1.0 + epsilons[j])
            cross_re = cross_re - (c_re * backs[j][0] + c_im * backs[j][1])
            cross_im = cross_im - (c_re * backs[j][1] - c_im * backs[j][0])
        if it == 2:
            (a_re, a_im), (b_re, b_im) = coefs
            pair_re, pair_im = a_re * b_re + a_im * b_im, a_re * b_im - a_im * b_re
            squared = squared + 2.0 * (pair_re * overlaps[0][0] - pair_im * overlaps[0][1])
        factor = 1.0 / jnp.sqrt(squared + 1e-06)
        alpha = (cross_re * factor, cross_im * factor)
        epsilon = 1e-06 * factor * factor
        if it == 1:
            over = (coefs[0][0] * epsilons[0] * factor, coefs[0][1] * epsilons[0] * factor)
            overlaps.append(over)
            backs[0] = (
                backs[0][0] - (alpha[0] * over[0] - alpha[1] * over[1]),
                backs[0][1] - (alpha[0] * over[1] + alpha[1] * over[0]),
            )
        backs.append((alpha[0] * epsilon, alpha[1] * epsilon))
        epsilons.append(epsilon)
        for site in range(sites):
            residual = residual_at(it, half, site)
            q = acc_ref[half, site]
            p = residual
            for j in range(it):
                q = q - times(coefs[j], basis_q[j, half, site])
                p = p - times(coefs[j], basis_p[j, half, site])
            q = q * factor
            p = p * factor
            if it < ITERS - 1:
                basis_q[it, half, site] = q
                basis_p[it, half, site] = p
            step = times(alpha, p)
            sol_half[half, site] = step if it == 0 else sol_half[half, site] + step
            res_half[half, site] = residual - times(alpha, q)

    for half in range(2):
        send_halo(0, half)
    for half in range(2):
        near_product(0, half)
    for it in range(ITERS):
        for half in range(2):
            far_product(it, half)
        for half in range(2):
            update(it, half)
            if it < ITERS - 1:
                send_halo(it + 1, half)
                near_product(it + 1, half)
    for from_ref, to_ref in ((sol_half, sol_ref), (res_half, res_ref)):
        for site in range(sites):
            first, second = from_ref[0, site], from_ref[1, site]
            low = lower_lanes(first.shape)
            to_ref[site, :comps] = jnp.where(low, first, swapped(second))
            to_ref[site, comps:] = jnp.where(low, swapped(first), second)

    for other in others[1:]:
        weights_copy(other, other, me).wait_send()
        for it in range(ITERS):
            for half in range(2):
                stat_copy(it, half, other, me).wait_send()
    part_copy(0).wait_send()

    for step in range(1, chips):
        part_copy(step).wait_send()
        source_copy(step, chip).wait_send()
    for it in range(ITERS):
        for half in range(2):
            for which in range(3):
                halo_copy(it, half, which).wait_send()


def shards_kernel(fine_source, projectors, stencil_links, quark_mass):
    count = lax.axis_size("ta")
    planes, local_columns, _, _, null, rhs = fine_source.shape
    sites, comps = stencil_links.shape[1], stencil_links.shape[2]
    rows = local_columns * 4 * null
    fine = fine_source.reshape(planes, rows, rhs)
    proj = projectors.reshape(count, local_columns, 4 * null * null)
    width = local_columns * comps
    links = stencil_links.reshape(sites, comps, 18 * comps)
    chips = count // 2
    vector = (sites, 2 * comps, rhs)
    f32, bf16 = jnp.float32, jnp.bfloat16
    dma = pltpu.SemaphoreType.DMA
    vmem = pl.BlockSpec(memory_space=pltpu.VMEM)
    hbm = pl.BlockSpec(memory_space=pl.ANY)
    parts = (chips, 2, comps, rhs)
    half = (sites, comps, rhs)
    sol, res = pl.pallas_call(
        functools.partial(solve_kernel, count, sites, comps),
        out_shape=[jax.ShapeDtypeStruct(vector, f32)] * 2,
        in_specs=[pl.BlockSpec(memory_space=pltpu.SMEM), vmem, hbm, hbm],
        out_specs=[vmem, vmem],
        scratch_shapes=[
            pltpu.VMEM(fine.shape, bf16),
            pltpu.VMEM(links.shape, bf16),
            pltpu.VMEM((sites, comps, 10 * comps), bf16),
            pltpu.VMEM((sites, comps, 4 * comps), bf16),
            pltpu.VMEM((sites, comps, 4 * comps), bf16),
            pltpu.VMEM((width, width), bf16),
            pltpu.VMEM((count, comps, width), bf16),
            pltpu.VMEM((count, comps, width), bf16),
            pltpu.VMEM(parts, f32),
            pltpu.VMEM(parts, f32),
            pltpu.VMEM(parts, f32),
            pltpu.VMEM(parts, f32),
            pltpu.VMEM((sites, 2, comps, rhs), f32),
            pltpu.VMEM((2, sites, 2 * comps, rhs), bf16),
            pltpu.VMEM((ITERS, 2, *half), bf16),
            pltpu.VMEM((ITERS, 2, 3, *half), bf16),
            pltpu.VMEM((2, *half), f32),
            pltpu.VMEM((2, *half), f32),
            pltpu.VMEM((2, *half), f32),
            pltpu.VMEM((ITERS - 1, 2, *half), f32),
            pltpu.VMEM((ITERS - 1, 2, *half), f32),
            pltpu.VMEM((ITERS, 2, 8, rhs), f32),
            pltpu.VMEM((ITERS, 2, count, 8, rhs), f32),
            dma((2,)),
            dma((count,)),
            dma((count,)),
            dma((chips,)),
            dma((chips,)),
            dma((chips,)),
            dma((chips,)),
            dma((ITERS, 2, 3)),
            dma((ITERS, 2, 3)),
            dma((ITERS, 2, count)),
            dma((ITERS, 2, count)),
        ],
        compiler_params=pltpu.CompilerParams(
            collective_id=0, has_side_effects=True, vmem_limit_bytes=60 * 1024 * 1024
        ),
    )(quark_mass, proj, fine, links)
    return sol.reshape(1, *vector), res.reshape(1, *vector)


def shards(fine_source, projectors, stencil_links, quark_mass):
    count = lax.axis_size("ta")
    sites = stencil_links.shape[1]
    local_columns = fine_source.shape[1]
    block = projectors.shape[1] // sites
    fits = (
        count == 2 * LZ
        and count == 2 * sites
        and count & (count - 1) == 0
        and block == 2 * local_columns
        and stencil_links.shape[2] % local_columns == 0
        and fine_source.shape[0] == count
        and ITERS == 3
        and fine_source.shape[5] % 2 == 0
    )
    chosen = shards_kernel if fits else shards_general
    return chosen(fine_source, projectors, stencil_links, quark_mass)


def solution(mesh):
    return jax.shard_map(
        shards,
        mesh=mesh,
        in_specs=(
            P("cfg", "ta", None, None, None, None),
            P(("cfg", "ta"), None, None),
            P(("cfg", "ta"), None, None, None),
            P("cfg"),
        ),
        out_specs=(P(("cfg", "ta"), None, None, None), P(("cfg", "ta"), None, None, None)),
        check_vma=False,
    )
```

profile of v0, /device:TPU:0, one launch (start us, length us, event | category | flops | bytes accessed | tf_op | source)
XLA Modules:
  0.0 83.4 jit_solution(18098745175990517030)
XLA Ops:
  1.3 78.6 %shard_map.59 = (f32[8,96,128]{2,1,0:T(8,128)}, f32[8,96,128]{2,1,0:T(8,128)}) custom-call(f32[1]{0:T(128)S(6)} %copy.8.mass_ref, bf16[16,8,2304]{2,1,0:T(8,128)(2,1)} %bitcast.7, bf16[16,768,128]{2,1,0:T(8,128)(2,1)} %bitcast.5, bf16[8,48,864]{2,1,0:T(8,128)(2,1)} %bitcast.6), custom_call_target="tpu_custom_call" | custom-call | tf_op jit(solution)/shard_map/pallas_call | solution.py:545
  79.8 1.8 %copy.9 = f32[1,8,96,128]{3,2,1,0:T(8,128)} copy(f32[1,8,96,128]{3,2,1,0:T(8,128)} %bitcast.9) | data formatting | bytes 786432
  81.6 1.8 %copy.10 = f32[1,8,96,128]{3,2,1,0:T(8,128)} copy(f32[1,8,96,128]{3,2,1,0:T(8,128)} %bitcast.8) | data formatting | bytes 786432
where the time goes:
time: 83.6 us; the launch traced here: 83.4 us
  Pallas kernels  78.6 us (94%)
  local copies, waits for them, and re-layouts  3.54 us (4%)
  between operations  1.29 us (2%)
    pallas_call x1, Pallas kernels, shards_kernel(): pl.pallas_call(functools.partial(solve_kernel, count, sites, comps), out_...  78.6 us
    unnamed x2, local copies, waits for them, and re-layouts  3.54 us

commit v1 on v0

--- a/solution.py
+++ b/solution.py
@@ -201,14 +201,40 @@
     return factor[0] * value + factor[1] * turned(value)
 
 
+def total_wait(region, sem):
+    pltpu.make_async_copy(region, region, sem).wait()
+
+
+def transposed(value, columns, comps):
+    row = lax.broadcasted_iota(jnp.int32, value.shape, 0)
+    chunk = lax.broadcasted_iota(jnp.int32, value.shape, 1) // comps
+    width = value.shape[1]
+    bits = columns.bit_length() - 1
+    for bit in range(bits):
+        size = 1 << bit
+        moved = pltpu.roll(value, width - size * comps, 1)
+        value = jnp.where((row // size) % 2 == 1, moved, value)
+    for bit in range(bits):
+        size = 1 << bit
+        moved = pltpu.roll(value, size, 0)
+        value = jnp.where((chunk // size) % 2 == 1, moved, value)
+    for bit in range(bits):
+        size = 1 << bit
+        moved = pltpu.roll(value, width - size * comps, 1)
+        value = jnp.where((row // size) % 2 == 1, moved, value)
+    return value
+
+
 def solve_kernel(
     count, sites, comps,
-    mass_ref, proj_ref, fine_hbm, links_hbm,
+    mass_ref, proj_hbm, fine_hbm, links_hbm,
     sol_ref, res_ref,
-    fine_ref, links_ref, near_ref, zlinks_ref, tlinks_ref, fold_ref,
-    weights_ref, weights_in, part_keep, part_out, part_in, sum_out, source_ref,
+    proj_ref, fine_ref, links_ref, near_ref, zlinks_ref, tlinks_ref,
+    weights_in, rights_ref, part_keep, part_out, part_in, sum_out, hi_out, source_ref,
+    first_round, first_z, first_t,
     wide_ref, round_ref, halo_ref, acc_ref, sol_half, res_half, basis_q, basis_p, stat_out, stat_in,
-    local_sem, wsend, wrecv, psend, precv, ssend, srecv, hsend, hrecv, gsend, grecv,
+    local_sem, wsend, wrecv, psend, precv, ssend, srecv, tsend, trecv, zsend, zrecv,
+    hsend, hrecv, gsend, grecv,
 ):
     me = lax.axis_index("ta")
     bits = count.bit_length() - 1
@@ -216,90 +242,79 @@
     chip = me // 2
     partner = chip * 2 + 1 - core
     chips = count // 2
+    far = chips // 2
     turns = [(1 - 2 * ((me // (1 << bit)) % 2)) * (1 << bit) for bit in range(bits)]
     others = [me]
     for step in range(1, count):
         top = step.bit_length() - 1
         others.append(others[step - (1 << top)] + turns[top])
     null = comps // 2
-    rows = fine_ref.shape[1]
     rhs = fine_ref.shape[2]
-
+    columns = proj_ref.shape[1]
+    width = columns * comps
+    groups = comps // columns
+
+    proj_copy = pltpu.make_async_copy(proj_hbm, proj_ref, local_sem.at[2])
+    proj_copy.start()
+    barrier = pltpu.get_barrier_semaphore()
+    for other in others[:0:-1]:
+        pl.semaphore_signal(barrier, inc=1, device_id={"ta": other}, device_id_type=MESH)
     fine_copy = pltpu.make_async_copy(fine_hbm, fine_ref, local_sem.at[0])
     fine_copy.start()
     links_copy = pltpu.make_async_copy(links_hbm, links_ref, local_sem.at[1])
     links_copy.start()
-
-    barrier = pltpu.get_barrier_semaphore()
-
-    for other in others[1:]:
-        pl.semaphore_signal(barrier, inc=1, device_id={"ta": other}, device_id_type=MESH)
+    proj_copy.wait()
     pl.semaphore_wait(barrier, count - 1)
 
-    def weights_copy(slot, other, origin):
+    def weights_copy(other, origin):
         return pltpu.make_async_remote_copy(
-            src_ref=weights_ref.at[slot], dst_ref=weights_in.at[origin],
-            send_sem=wsend.at[slot], recv_sem=wrecv.at[origin],
+            src_ref=proj_ref.at[other], dst_ref=weights_in.at[origin],
+            send_sem=wsend.at[0], recv_sem=wrecv.at[origin],
             device_id={"ta": other}, device_id_type=MESH,
         )
 
-    columns = proj_ref.shape[1]
-    width = columns * comps
-    groups = comps // columns
-    lane_at = lax.broadcasted_iota(jnp.int32, (columns, width), 1) // comps
-    row_at = lax.broadcasted_iota(jnp.int32, (columns, width), 0)
-    picks = (lane_at == row_at).astype(jnp.float32)
-    fold_row = lax.broadcasted_iota(jnp.int32, (width, width), 0) % comps
-    fold_lane = lax.broadcasted_iota(jnp.int32, (width, width), 1) % comps
-    fold_ref[...] = (fold_row == fold_lane).astype(jnp.float32).astype(jnp.bfloat16)
-
-    def arrange(slot):
-        raw = proj_ref[slot].astype(jnp.float32)
-        pieces = []
-        for column in range(columns):
-            for group in range(groups):
-                row = raw[column : column + 1, group * width : (group + 1) * width]
-                pieces.append(row * picks)
-        left = jnp.concatenate(pieces, axis=0).astype(jnp.bfloat16)
-        spread = jnp.dot(left, fold_ref[...], preferred_element_type=jnp.float32)
-        total = spread[:comps] * picks[0:1]
-        for column in range(1, columns):
-            block = spread[column * comps : (column + 1) * comps]
-            total = total + block * picks[column : column + 1]
-        weights_ref[slot] = total.astype(jnp.bfloat16)
-
-    def send_weights(step, carry):
-        other = flipped(me, count - 1 - step, bits)
-        arrange(other)
-        weights_copy(other, other, me).start()
+    order = list(range(1, 4)) + list(range(count // 2, count)) + list(range(4, count // 2))
+    for step in order:
+        weights_copy(others[step], me).start()
+
+    fine_copy.wait()
+
+    def build_right(plane, carry):
+        fine = fine_ref[plane].astype(jnp.float32).reshape(columns, 2, 2, null, rhs)
+        turned_order = [fine[(columns - at) % columns] for at in range(columns)]
+        for half in range(2):
+            picked = [
+                block[part, half] for block in turned_order for part in range(2)
+            ]
+            rights_ref[plane, :, half * rhs : (half + 1) * rhs] = jnp.concatenate(
+                picked, axis=0
+            ).astype(jnp.bfloat16)
         return carry
 
-    lax.fori_loop(0, count - 1, send_weights, 0)
-    arrange(me)
+    lax.fori_loop(0, count, build_right, 0)
 
     links_copy.wait()
     for site in range(sites):
         near_ref[site] = links_ref[site, :, : 10 * comps]
         zlinks_ref[site] = links_ref[site, :, 10 * comps : 14 * comps]
         tlinks_ref[site] = links_ref[site, :, 14 * comps : 18 * comps]
-    fine_copy.wait()
-
-    def restricted(plane, weights):
-        fine = fine_ref[plane].astype(jnp.float32).reshape(columns, 2, 2, null, rhs)
-
-        def ordered(real, imag, half):
-            view = jnp.stack([real[:, half], imag[:, half]], axis=1)
-            return view.reshape(width, rhs).astype(jnp.bfloat16)
-
-        real, imag = fine[:, 0], fine[:, 1]
-        right = jnp.concatenate(
-            [ordered(real, imag, 0), ordered(real, imag, 1),
-             ordered(imag, -real, 0), ordered(imag, -real, 1)], axis=1
-        )
-        total = jnp.dot(weights, right, preferred_element_type=jnp.float32)
-        real = jnp.concatenate([total[:null, :rhs], total[null:, rhs : 2 * rhs]], axis=0)
+
+    def restricted(plane, raw_ref):
+        raw = raw_ref[plane].astype(jnp.float32)
+        pieces = [
+            transposed(raw[:, group * width : (group + 1) * width], columns, comps)
+            for group in range(groups)
+        ]
+        upper = jnp.concatenate(pieces, axis=0)
+        lane = lax.broadcasted_iota(jnp.int32, upper.shape, 1) % comps
+        lower = jnp.where(
+            lane < null, -pltpu.roll(upper, width - null, 1), pltpu.roll(upper, null, 1)
+        )
+        left = jnp.concatenate([upper, lower], axis=0).astype(jnp.bfloat16)
+        total = jnp.dot(left, rights_ref[plane], preferred_element_type=jnp.float32)
+        real = jnp.concatenate([total[:null, :rhs], total[null:comps, rhs:]], axis=0)
         imag = jnp.concatenate(
-            [total[:null, 2 * rhs : 3 * rhs], total[null:, 3 * rhs :]], axis=0
+            [total[comps : comps + null, :rhs], total[comps + null :, rhs:]], axis=0
         )
         low = lower_lanes(real.shape)
         return jnp.stack(
@@ -309,52 +324,51 @@
     def part_copy(slot):
         return pltpu.make_async_remote_copy(
             src_ref=part_out.at[slot], dst_ref=part_in.at[slot],
-            send_sem=psend.at[slot], recv_sem=precv.at[slot],
+            send_sem=psend.at[0], recv_sem=precv.at[slot],
             device_id={"ta": partner}, device_id_type=MESH,
         )
 
     def source_copy(slot, origin):
         return pltpu.make_async_remote_copy(
             src_ref=sum_out.at[slot], dst_ref=source_ref.at[origin],
-            send_sem=ssend.at[slot], recv_sem=srecv.at[origin],
+            send_sem=ssend.at[0], recv_sem=srecv.at[origin],
             device_id={"ta": flipped(chip, slot, bits - 1) * 2 + core}, device_id_type=MESH,
+        )
+
+    def first_t_copy(slot):
+        return pltpu.make_async_remote_copy(
+            src_ref=hi_out.at[slot], dst_ref=first_t.at[chip],
+            send_sem=tsend.at[0], recv_sem=trecv.at[0],
+            device_id={"ta": (flipped(chip, slot, bits - 1) * 2 + core + count // 2) % count},
+            device_id_type=MESH,
         )
 
     def pair(step):
         other = flipped(chip, step, bits - 1)
         away = other * 2 + 1 - core
-        weights_copy(me, partner, away).wait_recv()
-        part_out[step] = restricted(away, weights_in[away])
+        weights_copy(partner, away).wait_recv()
+        part_out[step] = restricted(away, weights_in)
         part_copy(step).start()
         kept = other * 2 + core
-        weights_copy(me, partner, kept).wait_recv()
-        part_keep[step] = restricted(kept, weights_in[kept])
+        weights_copy(partner, kept).wait_recv()
+        part_keep[step] = restricted(kept, weights_in)
 
     def finish(step):
         part_copy(step).wait_recv()
-        sum_out[step] = part_keep[step] + part_in[step]
+        total = part_keep[step] + part_in[step]
+        rounded = total.astype(jnp.bfloat16)
+        sum_out[step] = total
         source_copy(step, chip).start()
 
-    weights_copy(me, partner, partner).wait_recv()
-    part_out[0] = restricted(partner, weights_in[partner])
-    part_copy(0).start()
-    part_keep[0] = restricted(me, weights_ref[me])
-    pair(1)
-    part_copy(0).wait_recv()
-    source_ref[chip] = part_keep[0] + part_in[0]
-
-    def pair_step(step, carry):
-        pair(step)
-        finish(step - 1)
-        return carry
-
-    lax.fori_loop(2, chips, pair_step, 0)
-    finish(chips - 1)
-
-    for step in range(1, chips):
-        source_copy(step, others[2 * step] // 2).wait_recv()
-
-    mass = mass_ref[0]
+        @pl.when(step != far)
+        def _():
+            hi_out[step] = rounded
+            first_t_copy(step).start()
+
+        @pl.when(step == far)
+        def _():
+            first_t[chip] = rounded
+
     base = (me // LZ) * LZ
     z_at = me % LZ
     above = base + (z_at + 1) % LZ
@@ -363,35 +377,85 @@
     targets = (other_time, above, below)
     lines = sites // LX
 
+    def first_z_copy(which, site):
+        return pltpu.make_async_remote_copy(
+            src_ref=first_round.at[site], dst_ref=first_z.at[which, site],
+            send_sem=zsend.at[0], recv_sem=zrecv.at[which],
+            device_id={"ta": targets[1 + which]}, device_id_type=MESH,
+        )
+
+    def forward(site):
+        first_round[site] = source_ref[site].astype(jnp.bfloat16)
+        for which in range(2):
+            first_z_copy(which, site).start()
+
+    weights_copy(partner, partner).wait_recv()
+    part_out[0] = restricted(partner, weights_in)
+    part_copy(0).start()
+    part_keep[0] = restricted(me, proj_ref)
+    pair(1)
+    part_copy(0).wait_recv()
+    own = part_keep[0] + part_in[0]
+    source_ref[chip] = own
+    hi_out[0] = own.astype(jnp.bfloat16)
+    first_t_copy(0).start()
+    forward(chip)
+
+    def pair_step(step, carry):
+        pair(step)
+        finish(step - 1)
+        return carry
+
+    lax.fori_loop(2, chips, pair_step, 0)
+    finish(chips - 1)
+
+    def forward_step(step, carry):
+        site = flipped(chip, step, bits - 1)
+        source_copy(0, site).wait_recv()
+        forward(site)
+        return carry
+
+    lax.fori_loop(1, chips, forward_step, 0)
+
+    mass = mass_ref[0]
+
     def place(site, dx, dy):
         return ((site // LX + dy) % lines) * LX + (site % LX + dx) % LX
 
     def halo_copy(it, half, which):
         return pltpu.make_async_remote_copy(
-            src_ref=round_ref.at[it, half], dst_ref=halo_ref.at[it, half, which],
-            send_sem=hsend.at[it, half, which], recv_sem=hrecv.at[it, half, which],
+            src_ref=round_ref.at[it - 1, half], dst_ref=halo_ref.at[it - 1, half, which],
+            send_sem=hsend.at[0], recv_sem=hrecv.at[it - 1, half, which],
             device_id={"ta": targets[which]}, device_id_type=MESH,
         )
 
-    def stat_copy(it, half, other, origin):
+    def stat_copy(it, half, other):
         return pltpu.make_async_remote_copy(
-            src_ref=stat_out.at[it, half], dst_ref=stat_in.at[it, half, origin],
-            send_sem=gsend.at[it, half, other], recv_sem=grecv.at[it, half, origin],
+            src_ref=stat_out.at[it, half], dst_ref=stat_in.at[it, half, me],
+            send_sem=gsend.at[0], recv_sem=grecv.at[it, half],
             device_id={"ta": other}, device_id_type=MESH,
         )
 
     def residual_at(it, half, site):
         return source_ref[site, half] if it == 0 else res_half[half, site]
 
+    def rounded_at(it, half, site):
+        return first_round[site, half] if it == 0 else round_ref[it - 1, half, site]
+
+    def halo_at(it, half, which, site):
+        if it > 0:
+            return halo_ref[it - 1, half, which, site]
+        return first_t[site, half] if which == 0 else first_z[which - 1, site, half]
+
     def send_halo(it, half):
         for site in range(sites):
-            round_ref[it, half, site] = residual_at(it, half, site).astype(jnp.bfloat16)
+            round_ref[it - 1, half, site] = res_half[half, site].astype(jnp.bfloat16)
         for which in range(3):
             halo_copy(it, half, which).start()
 
     def near_product(it, half):
         for site in range(sites):
-            wide_ref[half, site] = widened(round_ref[it, half, site])
+            wide_ref[half, site] = widened(rounded_at(it, half, site))
         steps = ((0, 0), (1, 0), (-1, 0), (0, 1), (0, -1))
         for site in range(sites):
             right = jnp.concatenate(
@@ -401,26 +465,42 @@
                 near_ref[site], right, preferred_element_type=jnp.float32
             )
 
+    def z_product(it, half, site):
+        right = jnp.concatenate(
+            [widened(halo_at(it, half, 2, site)), widened(halo_at(it, half, 1, site))], axis=0
+        )
+        return acc_ref[half, site] + jnp.dot(
+            zlinks_ref[site], right, preferred_element_type=jnp.float32
+        )
+
+    def t_product(it, half, site):
+        wide = widened(halo_at(it, half, 0, site))
+        right = jnp.concatenate([wide, wide], axis=0)
+        return acc_ref[half, site] + jnp.dot(
+            tlinks_ref[site], right, preferred_element_type=jnp.float32
+        )
+
     def far_product(it, half):
-        halo_copy(it, half, 2).wait_recv()
-        halo_copy(it, half, 1).wait_recv()
+        if it == 0:
+            if half == 0:
+                total_wait(first_t.at[pl.ds(0, sites - 1)], trecv.at[0])
+            first_part, last_part = t_product, z_product
+        else:
+            halo_copy(it, half, 2).wait_recv()
+            halo_copy(it, half, 1).wait_recv()
+            first_part, last_part = z_product, t_product
         for site in range(sites):
-            right = jnp.concatenate(
-                [widened(halo_ref[it, half, 2, site]), widened(halo_ref[it, half, 1, site])],
-                axis=0,
-            )
-            acc_ref[half, site] += jnp.dot(
-                zlinks_ref[site], right, preferred_element_type=jnp.float32
-            )
-        halo_copy(it, half, 0).wait_recv()
+            acc_ref[half, site] = first_part(it, half, site)
+        if it == 0:
+            if half == 0:
+                for which in range(2):
+                    total_wait(first_z.at[which], zrecv.at[which])
+        else:
+            halo_copy(it, half, 0).wait_recv()
         sums = [0.0] * (3 + 2 * it)
         for site in range(sites):
-            wide = widened(halo_ref[it, half, 0, site])
-            right = jnp.concatenate([wide, wide], axis=0)
-            product = acc_ref[half, site] + jnp.dot(
-                tlinks_ref[site], right, preferred_element_type=jnp.float32
-            )
-            q = product + mass * round_ref[it, half, site].astype(jnp.float32)
+            product = last_part(it, half, site)
+            q = product + mass * rounded_at(it, half, site).astype(jnp.float32)
             acc_ref[half, site] = q
             r = residual_at(it, half, site)
             q_other = swapped(q)
@@ -434,26 +514,35 @@
         lines_of = [jnp.sum(value, axis=0, keepdims=True) for value in sums]
         lines_of += [jnp.zeros((8 - len(lines_of), rhs), jnp.float32)]
         stats = jnp.concatenate(lines_of, axis=0)
-        stat_out[it, half] = stats
-
+        moved = swapped(stats)
+        low = lower_lanes(stats.shape)
+        reals = stats + moved
+        imags = jnp.where(low, stats - moved, moved - stats)
+        packed = jnp.concatenate(
+            [reals[0:1]]
+            + [
+                jnp.where(low[0:1], reals[at : at + 1], imags[at + 1 : at + 2])
+                for at in (1, 3, 5)
+            ],
+            axis=0,
+        )
+        stat_out[it, half] = packed
         for other in others[:0:-1]:
-            stat_copy(it, half, other, me).start()
-        stat_in[it, half, me] = stats
+            stat_copy(it, half, other).start()
+        stat_in[it, half, me] = packed
 
     scalars = [([], [], [], []) for _ in range(2)]
 
     def update(it, half):
-        for other in others[1:]:
-            stat_copy(it, half, other, other).wait_recv()
+        total_wait(stat_in.at[it, half, pl.ds(0, count - 1)], grecv.at[it, half])
         total = jnp.sum(stat_in[it, half], axis=0)
         moved = swapped(total)
-        reals = total + moved
-        imags = jnp.where(lower_lanes(total.shape), total - moved, moved - total)
+        low = lower_lanes(total.shape)
+        reals = jnp.where(low, total, moved)
+        imags = jnp.where(low, moved, total)
         backs, epsilons, overlaps, _ = scalars[half]
-        squared, cross_re, cross_im = reals[0:1], reals[1:2], imags[2:3]
-        coefs = [
-            (reals[3 + 2 * j : 4 + 2 * j], imags[4 + 2 * j : 5 + 2 * j]) for j in range(it)
-        ]
+        squared, cross_re, cross_im = reals[0:1], reals[1:2], imags[1:2]
+        coefs = [(reals[2 + j : 3 + j], imags[2 + j : 3 + j]) for j in range(it)]
         for j, (c_re, c_im) in enumerate(coefs):
             squared = squared - (c_re * c_re + c_im * c_im) * (1.0 + epsilons[j])
             cross_re = cross_re - (c_re * backs[j][0] + c_im * backs[j][1])
@@ -491,8 +580,6 @@
             res_half[half, site] = residual - times(alpha, q)
 
     for half in range(2):
-        send_halo(0, half)
-    for half in range(2):
         near_product(0, half)
     for it in range(ITERS):
         for half in range(2):
@@ -509,20 +596,13 @@
             to_ref[site, :comps] = jnp.where(low, first, swapped(second))
             to_ref[site, comps:] = jnp.where(low, swapped(first), second)
 
-    for other in others[1:]:
-        weights_copy(other, other, me).wait_send()
-        for it in range(ITERS):
-            for half in range(2):
-                stat_copy(it, half, other, me).wait_send()
-    part_copy(0).wait_send()
-
-    for step in range(1, chips):
-        part_copy(step).wait_send()
-        source_copy(step, chip).wait_send()
-    for it in range(ITERS):
-        for half in range(2):
-            for which in range(3):
-                halo_copy(it, half, which).wait_send()
+    total_wait(proj_ref.at[pl.ds(0, count - 1)], wsend.at[0])
+    total_wait(part_out, psend.at[0])
+    total_wait(sum_out.at[pl.ds(0, chips - 1)], ssend.at[0])
+    total_wait(hi_out.at[pl.ds(0, chips - 1)], tsend.at[0])
+    total_wait(first_z, zsend.at[0])
+    total_wait(halo_ref, hsend.at[0])
+    total_wait(stat_in.at[:, :, pl.ds(0, count - 1)], gsend.at[0])
 
 
 def shards_kernel(fine_source, projectors, stencil_links, quark_mass):
@@ -539,49 +619,57 @@
     f32, bf16 = jnp.float32, jnp.bfloat16
     dma = pltpu.SemaphoreType.DMA
     vmem = pl.BlockSpec(memory_space=pltpu.VMEM)
-    hbm = pl.BlockSpec(memory_space=pl.ANY)
+    hbm = pl.BlockSpec(memory_space=pltpu.HBM)
     parts = (chips, 2, comps, rhs)
     half = (sites, comps, rhs)
     sol, res = pl.pallas_call(
         functools.partial(solve_kernel, count, sites, comps),
-        out_shape=[jax.ShapeDtypeStruct(vector, f32)] * 2,
-        in_specs=[pl.BlockSpec(memory_space=pltpu.SMEM), vmem, hbm, hbm],
+        out_shape=[pltpu.VMEM(vector, f32)] * 2,
+        in_specs=[pl.BlockSpec(memory_space=pltpu.SMEM), hbm, hbm, hbm],
         out_specs=[vmem, vmem],
         scratch_shapes=[
+            pltpu.VMEM(proj.shape, bf16),
             pltpu.VMEM(fine.shape, bf16),
             pltpu.VMEM(links.shape, bf16),
             pltpu.VMEM((sites, comps, 10 * comps), bf16),
             pltpu.VMEM((sites, comps, 4 * comps), bf16),
             pltpu.VMEM((sites, comps, 4 * comps), bf16),
-            pltpu.VMEM((width, width), bf16),
-            pltpu.VMEM((count, comps, width), bf16),
-            pltpu.VMEM((count, comps, width), bf16),
+            pltpu.VMEM(proj.shape, bf16),
+            pltpu.VMEM((planes, width, 2 * rhs), bf16),
             pltpu.VMEM(parts, f32),
             pltpu.VMEM(parts, f32),
             pltpu.VMEM(parts, f32),
             pltpu.VMEM(parts, f32),
+            pltpu.VMEM(parts, bf16),
             pltpu.VMEM((sites, 2, comps, rhs), f32),
+            pltpu.VMEM((sites, 2, comps, rhs), bf16),
+            pltpu.VMEM((2, sites, 2, comps, rhs), bf16),
+            pltpu.VMEM((sites, 2, comps, rhs), bf16),
             pltpu.VMEM((2, sites, 2 * comps, rhs), bf16),
-            pltpu.VMEM((ITERS, 2, *half), bf16),
-            pltpu.VMEM((ITERS, 2, 3, *half), bf16),
+            pltpu.VMEM((ITERS - 1, 2, *half), bf16),
+            pltpu.VMEM((ITERS - 1, 2, 3, *half), bf16),
             pltpu.VMEM((2, *half), f32),
             pltpu.VMEM((2, *half), f32),
             pltpu.VMEM((2, *half), f32),
             pltpu.VMEM((ITERS - 1, 2, *half), f32),
             pltpu.VMEM((ITERS - 1, 2, *half), f32),
-            pltpu.VMEM((ITERS, 2, 8, rhs), f32),
-            pltpu.VMEM((ITERS, 2, count, 8, rhs), f32),
+            pltpu.VMEM((ITERS, 2, 4, rhs), f32),
+            pltpu.VMEM((ITERS, 2, count, 4, rhs), f32),
+            dma((3,)),
+            dma((1,)),
+            dma((count,)),
+            dma((1,)),
+            dma((chips,)),
+            dma((1,)),
+            dma((chips,)),
+            dma((1,)),
+            dma((1,)),
+            dma((1,)),
             dma((2,)),
-            dma((count,)),
-            dma((count,)),
-            dma((chips,)),
-            dma((chips,)),
-            dma((chips,)),
-            dma((chips,)),
-            dma((ITERS, 2, 3)),
-            dma((ITERS, 2, 3)),
-            dma((ITERS, 2, count)),
-            dma((ITERS, 2, count)),
+            dma((1,)),
+            dma((ITERS - 1, 2, 3)),
+            dma((1,)),
+            dma((ITERS, 2)),
         ],
         compiler_params=pltpu.CompilerParams(
             collective_id=0, has_side_effects=True, vmem_limit_bytes=60 * 1024 * 1024

time: 83.6 us -> 73.1 us (0.87)
  Pallas kernels: 78.6 us -> 70.2 us
  local copies, waits for them, and re-layouts: 3.54 us -> 1.49 us
    pallas_call x1, Pallas kernels: 78.6 us -> 70.2 us  [shards_kernel(): pl.pallas_call(functools.partial(solve_kernel, count, sites, comps), out_...]
    unnamed x2, local copies, waits for them, and re-layouts: 3.54 us -> 1.49 us
where the time goes in v1:
time: 73.1 us; the launch traced here: 73 us
  Pallas kernels  70.2 us (96%)
  local copies, waits for them, and re-layouts  1.49 us (2%)
  between operations  1.29 us (2%)
    pallas_call x1, Pallas kernels, shards_kernel(): pl.pallas_call(functools.partial(solve_kernel, count, sites, comps), out_...  70.2 us
    unnamed x2, local copies, waits for them, and re-layouts  1.49 us

profile of v1, /device:TPU:0, one launch (start us, length us, event | category | flops | bytes accessed | tf_op | source)
XLA Modules:
  0.0 73.0 jit_solution(2062266822112949501)
XLA Ops:
  1.3 70.2 %shard_map.59 = (f32[8,96,128]{2,1,0:T(8,128)S(1)}, f32[8,96,128]{2,1,0:T(8,128)S(1)}) custom-call(f32[1]{0:T(128)S(6)} %copy.10.mass_ref, bf16[16,8,2304]{2,1,0:T(8,128)(2,1)} %bitcast.9, bf16[16,768,128]{2,1,0:T(8,128)(2,1)} %bitcast.7, bf16[8,48,864]{2,1,0:T(8,128)(2,1)} %bitcast.8), custom_call_target="tpu_custom_call" | custom-call | tf_op jit(solution)/shard_map/pallas_call | solution.py:625
  71.5 0.7 %copy.8 = f32[1,8,96,128]{3,2,1,0:T(8,128)} copy(f32[1,8,96,128]{3,2,1,0:T(8,128)S(1)} %bitcast.6) | data formatting | bytes 786432
  72.2 0.7 %copy.9 = f32[1,8,96,128]{3,2,1,0:T(8,128)} copy(f32[1,8,96,128]{3,2,1,0:T(8,128)S(1)} %bitcast.5) | data formatting | bytes 786432

commit v2 on v1

--- a/solution.py
+++ b/solution.py
@@ -225,15 +225,31 @@
     return value
 
 
+CODE_SCALE = 2.0**12
+
+
+def coded(rest):
+    square = rest * rest * (CODE_SCALE * CODE_SCALE)
+    fourth = square * square
+    eighth = fourth * fourth
+    return jnp.where(rest < 0.0, -eighth, eighth).astype(jnp.bfloat16)
+
+
+def decoded(code):
+    value = code.astype(jnp.float32)
+    root = jnp.sqrt(jnp.sqrt(jnp.sqrt(jnp.abs(value)))) * (1.0 / CODE_SCALE)
+    return jnp.where(value < 0.0, -root, root)
+
+
 def solve_kernel(
     count, sites, comps,
     mass_ref, proj_hbm, fine_hbm, links_hbm,
     sol_ref, res_ref,
     proj_ref, fine_ref, links_ref, near_ref, zlinks_ref, tlinks_ref,
-    weights_in, rights_ref, part_keep, part_out, part_in, sum_out, hi_out, source_ref,
+    weights_in, rights_ref, part_keep, part_out, part_in, hi_out, lo_out, lo_in, source_ref,
     first_round, first_z, first_t,
     wide_ref, round_ref, halo_ref, acc_ref, sol_half, res_half, basis_q, basis_p, stat_out, stat_in,
-    local_sem, wsend, wrecv, psend, precv, ssend, srecv, tsend, trecv, zsend, zrecv,
+    local_sem, wsend, wrecv, psend, precv, ssend, srecv, tsend, trecv, lsend, lrecv, zsend, zrecv,
     hsend, hrecv, gsend, grecv,
 ):
     me = lax.axis_index("ta")
@@ -273,8 +289,14 @@
             device_id={"ta": other}, device_id_type=MESH,
         )
 
-    order = list(range(1, 4)) + list(range(count // 2, count)) + list(range(4, count // 2))
-    for step in order:
+    quarter = me // (count // 4)
+    outer = 1 - (quarter % 3 + 1) // 2
+    for step in range(1, 4):
+        weights_copy(others[step], me).start()
+    for step in range(count // 2, count):
+        crossed = step ^ (count // 4)
+        weights_copy(outer * others[step] + (1 - outer) * others[crossed], me).start()
+    for step in range(4, count // 2):
         weights_copy(others[step], me).start()
 
     fine_copy.wait()
@@ -328,46 +350,59 @@
             device_id={"ta": partner}, device_id_type=MESH,
         )
 
-    def source_copy(slot, origin):
+    def source_copy(slot, origin, half):
         return pltpu.make_async_remote_copy(
-            src_ref=sum_out.at[slot], dst_ref=source_ref.at[origin],
-            send_sem=ssend.at[0], recv_sem=srecv.at[origin],
+            src_ref=hi_out.at[slot, half], dst_ref=first_round.at[half, origin],
+            send_sem=ssend.at[0], recv_sem=srecv.at[half, origin],
             device_id={"ta": flipped(chip, slot, bits - 1) * 2 + core}, device_id_type=MESH,
         )
 
-    def first_t_copy(slot):
+    def rest_copy(slot, half):
         return pltpu.make_async_remote_copy(
-            src_ref=hi_out.at[slot], dst_ref=first_t.at[chip],
-            send_sem=tsend.at[0], recv_sem=trecv.at[0],
+            src_ref=lo_out.at[slot, half], dst_ref=lo_in.at[half, chip],
+            send_sem=lsend.at[0], recv_sem=lrecv.at[half],
+            device_id={"ta": flipped(chip, slot, bits - 1) * 2 + core}, device_id_type=MESH,
+        )
+
+    def first_t_copy(slot, half):
+        return pltpu.make_async_remote_copy(
+            src_ref=hi_out.at[slot, half], dst_ref=first_t.at[half, chip],
+            send_sem=tsend.at[0], recv_sem=trecv.at[half],
             device_id={"ta": (flipped(chip, slot, bits - 1) * 2 + core + count // 2) % count},
             device_id_type=MESH,
         )
+
+    def send_high(step, half):
+        source_copy(step, chip, half).start()
+
+        @pl.when(step != far)
+        def _():
+            first_t_copy(step, half).start()
 
     def pair(step):
         other = flipped(chip, step, bits - 1)
         away = other * 2 + 1 - core
+        kept = other * 2 + core
         weights_copy(partner, away).wait_recv()
-        part_out[step] = restricted(away, weights_in)
+        weights_copy(partner, kept).wait_recv()
+        sent, held = restricted(away, weights_in), restricted(kept, weights_in)
+        part_out[step] = sent
+        part_keep[step] = held
         part_copy(step).start()
-        kept = other * 2 + core
-        weights_copy(partner, kept).wait_recv()
-        part_keep[step] = restricted(kept, weights_in)
 
     def finish(step):
         part_copy(step).wait_recv()
         total = part_keep[step] + part_in[step]
         rounded = total.astype(jnp.bfloat16)
-        sum_out[step] = total
-        source_copy(step, chip).start()
-
-        @pl.when(step != far)
-        def _():
-            hi_out[step] = rounded
-            first_t_copy(step).start()
+        hi_out[step] = rounded
+        send_high(step, 0)
 
         @pl.when(step == far)
         def _():
-            first_t[chip] = rounded
+            first_t[0, chip] = rounded[0]
+            first_t[1, chip] = rounded[1]
+
+        lo_out[step] = coded(total - rounded.astype(jnp.float32))
 
     base = (me // LZ) * LZ
     z_at = me % LZ
@@ -377,45 +412,83 @@
     targets = (other_time, above, below)
     lines = sites // LX
 
-    def first_z_copy(which, site):
+    def first_z_copy(half, which, site):
         return pltpu.make_async_remote_copy(
-            src_ref=first_round.at[site], dst_ref=first_z.at[which, site],
-            send_sem=zsend.at[0], recv_sem=zrecv.at[which],
+            src_ref=first_round.at[half, site], dst_ref=first_z.at[half, which, site],
+            send_sem=zsend.at[0], recv_sem=zrecv.at[half, which],
             device_id={"ta": targets[1 + which]}, device_id_type=MESH,
         )
 
-    def forward(site):
-        first_round[site] = source_ref[site].astype(jnp.bfloat16)
+    def forward(half, site):
         for which in range(2):
-            first_z_copy(which, site).start()
+            first_z_copy(half, which, site).start()
 
     weights_copy(partner, partner).wait_recv()
-    part_out[0] = restricted(partner, weights_in)
+    sent, held = restricted(partner, weights_in), restricted(me, proj_ref)
+    part_out[0] = sent
+    part_keep[0] = held
     part_copy(0).start()
-    part_keep[0] = restricted(me, proj_ref)
     pair(1)
     part_copy(0).wait_recv()
     own = part_keep[0] + part_in[0]
-    source_ref[chip] = own
-    hi_out[0] = own.astype(jnp.bfloat16)
-    first_t_copy(0).start()
-    forward(chip)
-
-    def pair_step(step, carry):
-        pair(step)
-        finish(step - 1)
+    own_rounded = own.astype(jnp.bfloat16)
+    hi_out[0] = own_rounded
+    first_t_copy(0, 0).start()
+    for half in range(2):
+        source_ref[half, chip] = own[half]
+        first_round[half, chip] = own_rounded[half]
+    forward(0, chip)
+
+    def arranged(at):
+        group = at // 2
+        later = outer * ((2 * group + 1) % 3 + 1) + (1 - outer) * (group % 3 + 1)
+        return ((group + 2) // 3) * later * 2 + at % 2
+
+    def pair_step(at, carry):
+        pair(arranged(at))
+        finish(arranged(at - 1))
         return carry
 
     lax.fori_loop(2, chips, pair_step, 0)
-    finish(chips - 1)
-
-    def forward_step(step, carry):
-        site = flipped(chip, step, bits - 1)
-        source_copy(0, site).wait_recv()
-        forward(site)
-        return carry
-
-    lax.fori_loop(1, chips, forward_step, 0)
+    finish(arranged(chips - 1))
+
+    def rotated(at):
+        return (at + far - 1) % (chips - 1) + 1
+
+    def send_rest(half):
+        def rest_step(at, carry):
+            rest_copy(rotated(at), half).start()
+            return carry
+
+        lax.fori_loop(0, chips - 1, rest_step, 0)
+
+    def send_second():
+        def second_step(at, carry):
+            send_high(rotated(at), 1)
+            return carry
+
+        first_t_copy(0, 1).start()
+        forward(1, chip)
+        lax.fori_loop(0, chips - 1, second_step, 0)
+
+    def forward_all(half):
+        def forward_step(at, carry):
+            site = flipped(chip, arranged(at), bits - 1)
+            source_copy(0, site, half).wait_recv()
+            forward(half, site)
+            return carry
+
+        lax.fori_loop(1, chips, forward_step, 0)
+
+    def complete_source(half):
+        def complete_step(step, carry):
+            site = flipped(chip, step, bits - 1)
+            high = first_round[half, site].astype(jnp.float32)
+            source_ref[half, site] = high + decoded(lo_in[half, site])
+            return carry
+
+        total_wait(lo_in.at[half, pl.ds(0, sites - 1)], lrecv.at[half])
+        lax.fori_loop(1, chips, complete_step, 0)
 
     mass = mass_ref[0]
 
@@ -437,21 +510,30 @@
         )
 
     def residual_at(it, half, site):
-        return source_ref[site, half] if it == 0 else res_half[half, site]
+        return source_ref[half, site] if it == 0 else res_half[half, site]
 
     def rounded_at(it, half, site):
-        return first_round[site, half] if it == 0 else round_ref[it - 1, half, site]
+        return first_round[half, site] if it == 0 else round_ref[it - 1, half, site]
 
     def halo_at(it, half, which, site):
         if it > 0:
             return halo_ref[it - 1, half, which, site]
-        return first_t[site, half] if which == 0 else first_z[which - 1, site, half]
+        return first_t[half, site] if which == 0 else first_z[half, which - 1, site]
 
     def send_halo(it, half):
         for site in range(sites):
             round_ref[it - 1, half, site] = res_half[half, site].astype(jnp.bfloat16)
-        for which in range(3):
+        @pl.when(outer == 0)
+        def _():
+            halo_copy(it, half, 0).start()
+
+        for which in range(1, 3):
             halo_copy(it, half, which).start()
+
+    def send_late_halo(it, half):
+        @pl.when(outer == 1)
+        def _():
+            halo_copy(it, half, 0).start()
 
     def near_product(it, half):
         for site in range(sites):
@@ -480,37 +562,49 @@
             tlinks_ref[site], right, preferred_element_type=jnp.float32
         )
 
+    def full_product(it, half, site, product):
+        return product + mass * rounded_at(it, half, site).astype(jnp.float32)
+
+    def add_sums(it, half, site, q, sums):
+        r = residual_at(it, half, site)
+        q_other = swapped(q)
+        sums[0] += q * q
+        sums[1] += q * r
+        sums[2] += q * swapped(r)
+        for j in range(it):
+            b = basis_q[j, half, site]
+            sums[3 + 2 * j] += b * q
+            sums[4 + 2 * j] += b * q_other
+
+    def first_t_product(half):
+        total_wait(first_t.at[half, pl.ds(0, sites - 1)], trecv.at[half])
+        for site in range(sites):
+            acc_ref[half, site] = t_product(0, half, site)
+
+    def first_z_product(half):
+        for which in range(2):
+            total_wait(first_z.at[half, which], zrecv.at[half, which])
+        sums = [0.0] * 3
+        for site in range(sites):
+            q = full_product(0, half, site, z_product(0, half, site))
+            acc_ref[half, site] = q
+            add_sums(0, half, site, q, sums)
+        send_stats(0, half, sums)
+
     def far_product(it, half):
-        if it == 0:
-            if half == 0:
-                total_wait(first_t.at[pl.ds(0, sites - 1)], trecv.at[0])
-            first_part, last_part = t_product, z_product
-        else:
-            halo_copy(it, half, 2).wait_recv()
-            halo_copy(it, half, 1).wait_recv()
-            first_part, last_part = z_product, t_product
+        halo_copy(it, half, 2).wait_recv()
+        halo_copy(it, half, 1).wait_recv()
         for site in range(sites):
-            acc_ref[half, site] = first_part(it, half, site)
-        if it == 0:
-            if half == 0:
-                for which in range(2):
-                    total_wait(first_z.at[which], zrecv.at[which])
-        else:
-            halo_copy(it, half, 0).wait_recv()
+            acc_ref[half, site] = z_product(it, half, site)
+        halo_copy(it, half, 0).wait_recv()
         sums = [0.0] * (3 + 2 * it)
         for site in range(sites):
-            product = last_part(it, half, site)
-            q = product + mass * rounded_at(it, half, site).astype(jnp.float32)
+            q = full_product(it, half, site, t_product(it, half, site))
             acc_ref[half, site] = q
-            r = residual_at(it, half, site)
-            q_other = swapped(q)
-            sums[0] += q * q
-            sums[1] += q * r
-            sums[2] += q * swapped(r)
-            for j in range(it):
-                b = basis_q[j, half, site]
-                sums[3 + 2 * j] += b * q
-                sums[4 + 2 * j] += b * q_other
+            add_sums(it, half, site, q, sums)
+        send_stats(it, half, sums)
+
+    def send_stats(it, half, sums):
         lines_of = [jnp.sum(value, axis=0, keepdims=True) for value in sums]
         lines_of += [jnp.zeros((8 - len(lines_of), rhs), jnp.float32)]
         stats = jnp.concatenate(lines_of, axis=0)
@@ -579,16 +673,38 @@
             sol_half[half, site] = step if it == 0 else sol_half[half, site] + step
             res_half[half, site] = residual - times(alpha, q)
 
-    for half in range(2):
-        near_product(0, half)
+    pl.when(outer == 0)(lambda: send_rest(0))
+    forward_all(0)
+    pl.when(outer == 1)(lambda: send_rest(0))
+    @pl.when(outer == 0)
+    def _():
+        send_second()
+        send_rest(1)
+
+    near_product(0, 0)
+    first_t_product(0)
+    @pl.when(outer == 1)
+    def _():
+        send_second()
+        send_rest(1)
+
+    complete_source(0)
+    forward_all(1)
+    first_z_product(0)
+    near_product(0, 1)
+    first_t_product(1)
+    complete_source(1)
+    first_z_product(1)
     for it in range(ITERS):
-        for half in range(2):
-            far_product(it, half)
+        if it > 0:
+            for half in range(2):
+                far_product(it, half)
         for half in range(2):
             update(it, half)
             if it < ITERS - 1:
                 send_halo(it + 1, half)
                 near_product(it + 1, half)
+                send_late_halo(it + 1, half)
     for from_ref, to_ref in ((sol_half, sol_ref), (res_half, res_ref)):
         for site in range(sites):
             first, second = from_ref[0, site], from_ref[1, site]
@@ -598,7 +714,8 @@
 
     total_wait(proj_ref.at[pl.ds(0, count - 1)], wsend.at[0])
     total_wait(part_out, psend.at[0])
-    total_wait(sum_out.at[pl.ds(0, chips - 1)], ssend.at[0])
+    total_wait(hi_out.at[pl.ds(0, chips - 1)], ssend.at[0])
+    total_wait(lo_out.at[pl.ds(0, chips - 1)], lsend.at[0])
     total_wait(hi_out.at[pl.ds(0, chips - 1)], tsend.at[0])
     total_wait(first_z, zsend.at[0])
     total_wait(halo_ref, hsend.at[0])
@@ -639,12 +756,13 @@
             pltpu.VMEM(parts, f32),
             pltpu.VMEM(parts, f32),
             pltpu.VMEM(parts, f32),
-            pltpu.VMEM(parts, f32),
             pltpu.VMEM(parts, bf16),
-            pltpu.VMEM((sites, 2, comps, rhs), f32),
-            pltpu.VMEM((sites, 2, comps, rhs), bf16),
-            pltpu.VMEM((2, sites, 2, comps, rhs), bf16),
-            pltpu.VMEM((sites, 2, comps, rhs), bf16),
+            pltpu.VMEM(parts, bf16),
+            pltpu.VMEM((2, sites, comps, rhs), bf16),
+            pltpu.VMEM((2, sites, comps, rhs), f32),
+            pltpu.VMEM((2, sites, comps, rhs), bf16),
+            pltpu.VMEM((2, 2, sites, comps, rhs), bf16),
+            pltpu.VMEM((2, sites, comps, rhs), bf16),
             pltpu.VMEM((2, sites, 2 * comps, rhs), bf16),
             pltpu.VMEM((ITERS - 1, 2, *half), bf16),
             pltpu.VMEM((ITERS - 1, 2, 3, *half), bf16),
@@ -661,11 +779,13 @@
             dma((1,)),
             dma((chips,)),
             dma((1,)),
-            dma((chips,)),
-            dma((1,)),
-            dma((1,)),
+            dma((2, chips)),
             dma((1,)),
             dma((2,)),
+            dma((1,)),
+            dma((2,)),
+            dma((1,)),
+            dma((2, 2)),
             dma((1,)),
             dma((ITERS - 1, 2, 3)),
             dma((1,)),

time: 73.1 us -> 70.9 us (0.970)
  Pallas kernels: 70.2 us -> 68 us
    pallas_call x1, Pallas kernels: 70.2 us -> 68 us  [shards_kernel(): pl.pallas_call(functools.partial(solve_kernel, count, sites, comps), out_...]
where the time goes in v2:
time: 70.9 us; the launch traced here: 70.7 us
  Pallas kernels  68 us (96%)
  local copies, waits for them, and re-layouts  1.49 us (2%)
  between operations  1.29 us (2%)
    pallas_call x1, Pallas kernels, shards_kernel(): pl.pallas_call(functools.partial(solve_kernel, count, sites, comps), out_...  68 us
    unnamed x2, local copies, waits for them, and re-layouts  1.49 us

profile of v2, /device:TPU:0, one launch (start us, length us, event | category | flops | bytes accessed | tf_op | source)
XLA Modules:
  0.0 70.7 jit_solution(13911814016542083737)
XLA Ops:
  1.3 68.0 %shard_map.59 = (f32[8,96,128]{2,1,0:T(8,128)S(1)}, f32[8,96,128]{2,1,0:T(8,128)S(1)}) custom-call(f32[1]{0:T(128)S(6)} %copy.10.mass_ref, bf16[16,8,2304]{2,1,0:T(8,128)(2,1)} %bitcast.9, bf16[16,768,128]{2,1,0:T(8,128)(2,1)} %bitcast.7, bf16[8,48,864]{2,1,0:T(8,128)(2,1)} %bitcast.8), custom_call_target="tpu_custom_call" | custom-call | tf_op jit(solution)/shard_map/pallas_call | solution.py:742
  69.2 0.7 %copy.8 = f32[1,8,96,128]{3,2,1,0:T(8,128)} copy(f32[1,8,96,128]{3,2,1,0:T(8,128)S(1)} %bitcast.6) | data formatting | bytes 786432
  70.0 0.7 %copy.9 = f32[1,8,96,128]{3,2,1,0:T(8,128)} copy(f32[1,8,96,128]{3,2,1,0:T(8,128)S(1)} %bitcast.5) | data formatting | bytes 786432

commit v3 on v2

--- a/solution.py
+++ b/solution.py
@@ -350,10 +350,10 @@
             device_id={"ta": partner}, device_id_type=MESH,
         )
 
-    def source_copy(slot, origin, half):
+    def source_copy(slot, origin):
         return pltpu.make_async_remote_copy(
-            src_ref=hi_out.at[slot, half], dst_ref=first_round.at[half, origin],
-            send_sem=ssend.at[0], recv_sem=srecv.at[half, origin],
+            src_ref=hi_out.at[slot], dst_ref=first_round.at[origin],
+            send_sem=ssend.at[0], recv_sem=srecv.at[origin],
             device_id={"ta": flipped(chip, slot, bits - 1) * 2 + core}, device_id_type=MESH,
         )
 
@@ -361,23 +361,15 @@
         return pltpu.make_async_remote_copy(
             src_ref=lo_out.at[slot, half], dst_ref=lo_in.at[half, chip],
             send_sem=lsend.at[0], recv_sem=lrecv.at[half],
-            device_id={"ta": flipped(chip, slot, bits - 1) * 2 + core}, device_id_type=MESH,
+            device_id={"ta": others[2 * slot]}, device_id_type=MESH,
         )
 
     def first_t_copy(slot, half):
         return pltpu.make_async_remote_copy(
             src_ref=hi_out.at[slot, half], dst_ref=first_t.at[half, chip],
             send_sem=tsend.at[0], recv_sem=trecv.at[half],
-            device_id={"ta": (flipped(chip, slot, bits - 1) * 2 + core + count // 2) % count},
-            device_id_type=MESH,
-        )
-
-    def send_high(step, half):
-        source_copy(step, chip, half).start()
-
-        @pl.when(step != far)
-        def _():
-            first_t_copy(step, half).start()
+            device_id={"ta": others[2 * (slot ^ far)]}, device_id_type=MESH,
+        )
 
     def pair(step):
         other = flipped(chip, step, bits - 1)
@@ -395,13 +387,7 @@
         total = part_keep[step] + part_in[step]
         rounded = total.astype(jnp.bfloat16)
         hi_out[step] = rounded
-        send_high(step, 0)
-
-        @pl.when(step == far)
-        def _():
-            first_t[0, chip] = rounded[0]
-            first_t[1, chip] = rounded[1]
-
+        source_copy(step, chip).start()
         lo_out[step] = coded(total - rounded.astype(jnp.float32))
 
     base = (me // LZ) * LZ
@@ -412,16 +398,16 @@
     targets = (other_time, above, below)
     lines = sites // LX
 
-    def first_z_copy(half, which, site):
+    def first_z_copy(which, site):
         return pltpu.make_async_remote_copy(
-            src_ref=first_round.at[half, site], dst_ref=first_z.at[half, which, site],
-            send_sem=zsend.at[0], recv_sem=zrecv.at[half, which],
+            src_ref=first_round.at[site], dst_ref=first_z.at[which, site],
+            send_sem=zsend.at[0], recv_sem=zrecv.at[which],
             device_id={"ta": targets[1 + which]}, device_id_type=MESH,
         )
 
-    def forward(half, site):
+    def forward(site):
         for which in range(2):
-            first_z_copy(half, which, site).start()
+            first_z_copy(which, site).start()
 
     weights_copy(partner, partner).wait_recv()
     sent, held = restricted(partner, weights_in), restricted(me, proj_ref)
@@ -433,11 +419,10 @@
     own = part_keep[0] + part_in[0]
     own_rounded = own.astype(jnp.bfloat16)
     hi_out[0] = own_rounded
-    first_t_copy(0, 0).start()
+    first_round[chip] = own_rounded
     for half in range(2):
         source_ref[half, chip] = own[half]
-        first_round[half, chip] = own_rounded[half]
-    forward(0, chip)
+    forward(chip)
 
     def arranged(at):
         group = at // 2
@@ -452,30 +437,21 @@
     lax.fori_loop(2, chips, pair_step, 0)
     finish(arranged(chips - 1))
 
-    def rotated(at):
-        return (at + far - 1) % (chips - 1) + 1
+    def send_after(half):
+        first_t[half, chip] = hi_out[far, half]
+        for step in range(chips - 1, -1, -1):
+            if step != far:
+                first_t_copy(step, half).start()
 
     def send_rest(half):
-        def rest_step(at, carry):
-            rest_copy(rotated(at), half).start()
-            return carry
-
-        lax.fori_loop(0, chips - 1, rest_step, 0)
-
-    def send_second():
-        def second_step(at, carry):
-            send_high(rotated(at), 1)
-            return carry
-
-        first_t_copy(0, 1).start()
-        forward(1, chip)
-        lax.fori_loop(0, chips - 1, second_step, 0)
-
-    def forward_all(half):
+        for step in range(chips - 1, 0, -1):
+            rest_copy(step, half).start()
+
+    def forward_all():
         def forward_step(at, carry):
             site = flipped(chip, arranged(at), bits - 1)
-            source_copy(0, site, half).wait_recv()
-            forward(half, site)
+            source_copy(0, site).wait_recv()
+            forward(site)
             return carry
 
         lax.fori_loop(1, chips, forward_step, 0)
@@ -483,7 +459,7 @@
     def complete_source(half):
         def complete_step(step, carry):
             site = flipped(chip, step, bits - 1)
-            high = first_round[half, site].astype(jnp.float32)
+            high = first_round[site, half].astype(jnp.float32)
             source_ref[half, site] = high + decoded(lo_in[half, site])
             return carry
 
@@ -495,12 +471,27 @@
     def place(site, dx, dy):
         return ((site // LX + dy) % lines) * LX + (site % LX + dx) % LX
 
-    def halo_copy(it, half, which):
+    pieces = 2
+    span = sites // pieces
+
+    def z_copy(it, half, which):
         return pltpu.make_async_remote_copy(
             src_ref=round_ref.at[it - 1, half], dst_ref=halo_ref.at[it - 1, half, which],
-            send_sem=hsend.at[0], recv_sem=hrecv.at[it - 1, half, which],
+            send_sem=hsend.at[0], recv_sem=hrecv.at[half, which - 1],
             device_id={"ta": targets[which]}, device_id_type=MESH,
         )
+
+    def t_copy(it, half, piece):
+        part = pl.ds(piece * span, span)
+        return pltpu.make_async_remote_copy(
+            src_ref=round_ref.at[it - 1, half, part], dst_ref=halo_ref.at[it - 1, half, 0, part],
+            send_sem=hsend.at[0], recv_sem=hrecv.at[half, 2 + piece],
+            device_id={"ta": other_time}, device_id_type=MESH,
+        )
+
+    def send_t(it, half):
+        for piece in range(pieces):
+            t_copy(it, half, piece).start()
 
     def stat_copy(it, half, other):
         return pltpu.make_async_remote_copy(
@@ -513,27 +504,22 @@
         return source_ref[half, site] if it == 0 else res_half[half, site]
 
     def rounded_at(it, half, site):
-        return first_round[half, site] if it == 0 else round_ref[it - 1, half, site]
+        return first_round[site, half] if it == 0 else round_ref[it - 1, half, site]
 
     def halo_at(it, half, which, site):
         if it > 0:
             return halo_ref[it - 1, half, which, site]
-        return first_t[half, site] if which == 0 else first_z[half, which - 1, site]
+        return first_t[half, site] if which == 0 else first_z[which - 1, site, half]
 
     def send_halo(it, half):
         for site in range(sites):
             round_ref[it - 1, half, site] = res_half[half, site].astype(jnp.bfloat16)
-        @pl.when(outer == 0)
-        def _():
-            halo_copy(it, half, 0).start()
-
+        pl.when(outer == 0)(lambda: send_t(it, half))
         for which in range(1, 3):
-            halo_copy(it, half, which).start()
+            z_copy(it, half, which).start()
 
     def send_late_halo(it, half):
-        @pl.when(outer == 1)
-        def _():
-            halo_copy(it, half, 0).start()
+        pl.when(outer == 1)(lambda: send_t(it, half))
 
     def near_product(it, half):
         for site in range(sites):
@@ -582,8 +568,9 @@
             acc_ref[half, site] = t_product(0, half, site)
 
     def first_z_product(half):
-        for which in range(2):
-            total_wait(first_z.at[half, which], zrecv.at[half, which])
+        if half == 0:
+            for which in range(2):
+                total_wait(first_z.at[which], zrecv.at[which])
         sums = [0.0] * 3
         for site in range(sites):
             q = full_product(0, half, site, z_product(0, half, site))
@@ -592,14 +579,16 @@
         send_stats(0, half, sums)
 
     def far_product(it, half):
-        halo_copy(it, half, 2).wait_recv()
-        halo_copy(it, half, 1).wait_recv()
+        for which in (2, 1):
+            z_copy(it, half, which).wait_recv()
         for site in range(sites):
-            acc_ref[half, site] = z_product(it, half, site)
-        halo_copy(it, half, 0).wait_recv()
+            product = z_product(it, half, site)
+            acc_ref[half, site] = full_product(it, half, site, product)
         sums = [0.0] * (3 + 2 * it)
         for site in range(sites):
-            q = full_product(it, half, site, t_product(it, half, site))
+            if site % span == 0:
+                t_copy(it, half, site // span).wait_recv()
+            q = t_product(it, half, site)
             acc_ref[half, site] = q
             add_sums(it, half, site, q, sums)
         send_stats(it, half, sums)
@@ -670,28 +659,31 @@
                 basis_q[it, half, site] = q
                 basis_p[it, half, site] = p
             step = times(alpha, p)
-            sol_half[half, site] = step if it == 0 else sol_half[half, site] + step
-            res_half[half, site] = residual - times(alpha, q)
-
+            new_sol = step if it == 0 else sol_half[half, site] + step
+            new_res = residual - times(alpha, q)
+            if it < ITERS - 1 or half == 0:
+                sol_half[half, site] = new_sol
+                res_half[half, site] = new_res
+            else:
+                unpack(sol_ref, site, sol_half[0, site], new_sol)
+                unpack(res_ref, site, res_half[0, site], new_res)
+
+    def unpack(to_ref, site, first, second):
+        low = lower_lanes(first.shape)
+        to_ref[site, :comps] = jnp.where(low, first, swapped(second))
+        to_ref[site, comps:] = jnp.where(low, swapped(first), second)
+
+    send_after(0)
     pl.when(outer == 0)(lambda: send_rest(0))
-    forward_all(0)
+    forward_all()
     pl.when(outer == 1)(lambda: send_rest(0))
-    @pl.when(outer == 0)
-    def _():
-        send_second()
-        send_rest(1)
-
     near_product(0, 0)
+    near_product(0, 1)
     first_t_product(0)
-    @pl.when(outer == 1)
-    def _():
-        send_second()
-        send_rest(1)
-
+    send_after(1)
+    send_rest(1)
     complete_source(0)
-    forward_all(1)
     first_z_product(0)
-    near_product(0, 1)
     first_t_product(1)
     complete_source(1)
     first_z_product(1)
@@ -705,13 +697,6 @@
                 send_halo(it + 1, half)
                 near_product(it + 1, half)
                 send_late_halo(it + 1, half)
-    for from_ref, to_ref in ((sol_half, sol_ref), (res_half, res_ref)):
-        for site in range(sites):
-            first, second = from_ref[0, site], from_ref[1, site]
-            low = lower_lanes(first.shape)
-            to_ref[site, :comps] = jnp.where(low, first, swapped(second))
-            to_ref[site, comps:] = jnp.where(low, swapped(first), second)
-
     total_wait(proj_ref.at[pl.ds(0, count - 1)], wsend.at[0])
     total_wait(part_out, psend.at[0])
     total_wait(hi_out.at[pl.ds(0, chips - 1)], ssend.at[0])
@@ -720,6 +705,30 @@
     total_wait(first_z, zsend.at[0])
     total_wait(halo_ref, hsend.at[0])
     total_wait(stat_in.at[:, :, pl.ds(0, count - 1)], gsend.at[0])
+
+
+def store_kernel(sol_ref, res_ref, sol_hbm, res_hbm, sems):
+    copies = [
+        pltpu.make_async_copy(from_ref, to_ref, sems.at[at])
+        for at, (from_ref, to_ref) in enumerate(((sol_ref, sol_hbm), (res_ref, res_hbm)))
+    ]
+    for copy in copies:
+        copy.start()
+    for copy in copies:
+        copy.wait()
+
+
+def stored(sol, res):
+    vmem = pl.BlockSpec(memory_space=pltpu.VMEM)
+    hbm = pl.BlockSpec(memory_space=pltpu.HBM)
+    return pl.pallas_call(
+        store_kernel,
+        out_shape=[jax.ShapeDtypeStruct(value.shape, value.dtype) for value in (sol, res)],
+        in_specs=[vmem, vmem],
+        out_specs=[hbm, hbm],
+        scratch_shapes=[pltpu.SemaphoreType.DMA((2,))],
+        compiler_params=pltpu.CompilerParams(vmem_limit_bytes=1024 * 1024),
+    )(sol, res)
 
 
 def shards_kernel(fine_source, projectors, stencil_links, quark_mass):
@@ -760,8 +769,8 @@
             pltpu.VMEM(parts, bf16),
             pltpu.VMEM((2, sites, comps, rhs), bf16),
             pltpu.VMEM((2, sites, comps, rhs), f32),
-            pltpu.VMEM((2, sites, comps, rhs), bf16),
-            pltpu.VMEM((2, 2, sites, comps, rhs), bf16),
+            pltpu.VMEM((sites, 2, comps, rhs), bf16),
+            pltpu.VMEM((2, sites, 2, comps, rhs), bf16),
             pltpu.VMEM((2, sites, comps, rhs), bf16),
             pltpu.VMEM((2, sites, 2 * comps, rhs), bf16),
             pltpu.VMEM((ITERS - 1, 2, *half), bf16),
@@ -779,15 +788,15 @@
             dma((1,)),
             dma((chips,)),
             dma((1,)),
-            dma((2, chips)),
+            dma((chips,)),
             dma((1,)),
             dma((2,)),
             dma((1,)),
             dma((2,)),
             dma((1,)),
-            dma((2, 2)),
+            dma((2,)),
             dma((1,)),
-            dma((ITERS - 1, 2, 3)),
+            dma((2, 4)),
             dma((1,)),
             dma((ITERS, 2)),
         ],
@@ -795,6 +804,7 @@
             collective_id=0, has_side_effects=True, vmem_limit_bytes=60 * 1024 * 1024
         ),
     )(quark_mass, proj, fine, links)
+    sol, res = stored(sol, res)
     return sol.reshape(1, *vector), res.reshape(1, *vector)
 
 

time: 70.9 us -> 68.9 us (0.972)
  local copies, waits for them, and re-layouts: 1.49 us -> 0 us
    unnamed x2 -> x0, local copies, waits for them, and re-layouts: 1.49 us -> none
    pallas_call x1, Pallas kernels: 68 us -> 66.6 us  [shards_kernel(): pl.pallas_call(functools.partial(solve_kernel, count, sites, comps), out_...]
    pallas_call x0 -> x1, Pallas kernels: none -> 0.89 us  [stored(): pl.pallas_call(store_kernel, out_shape=[jax.ShapeDtypeStruct(value.shape,...]
where the time goes in v3:
time: 68.9 us; the launch traced here: 68.8 us
  Pallas kernels  67.5 us (98%)
  between operations  1.29 us (2%)
    pallas_call x1, Pallas kernels, shards_kernel(): pl.pallas_call(functools.partial(solve_kernel, count, sites, comps), out_...  66.6 us

profile of v3, /device:TPU:0, one launch (start us, length us, event | category | flops | bytes accessed | tf_op | source)
XLA Modules:
  0.0 68.8 jit_solution(12095139490329366061)
XLA Ops:
  1.3 66.6 %shard_map.59 = (f32[8,96,128]{2,1,0:T(8,128)S(1)}, f32[8,96,128]{2,1,0:T(8,128)S(1)}) custom-call(f32[1]{0:T(128)S(6)} %copy.6.mass_ref, bf16[16,8,2304]{2,1,0:T(8,128)(2,1)} %bitcast.7, bf16[16,768,128]{2,1,0:T(8,128)(2,1)} %bitcast.5, bf16[8,48,864]{2,1,0:T(8,128)(2,1)} %bitcast.6), custom_call_target="tpu_custom_call" | custom-call | tf_op jit(solution)/shard_map/pallas_call | solution.py:751
  67.9 0.9 %shard_map.60 = (f32[8,96,128]{2,1,0:T(8,128)}, f32[8,96,128]{2,1,0:T(8,128)}) custom-call(f32[8,96,128]{2,1,0:T(8,128)S(1)} %get-tuple-element.6.sol_ref, f32[8,96,128]{2,1,0:T(8,128)S(1)} %get-tuple-element.7.res_ref), custom_call_target="tpu_custom_call" | custom-call | tf_op jit(solution)/shard_map/pallas_call | solution.py:724

commit v4 on v3

--- a/solution.py
+++ b/solution.py
@@ -248,7 +248,8 @@
     proj_ref, fine_ref, links_ref, near_ref, zlinks_ref, tlinks_ref,
     weights_in, rights_ref, part_keep, part_out, part_in, hi_out, lo_out, lo_in, source_ref,
     first_round, first_z, first_t,
-    wide_ref, round_ref, halo_ref, acc_ref, sol_half, res_half, basis_q, basis_p, stat_out, stat_in,
+    wide_ref, round_ref, halo_ref, acc_ref, acc_turned, sol_half, res_half, res_turned,
+    basis_q, basis_p, turned_q, turned_p, stat_out, stat_in,
     local_sem, wsend, wrecv, psend, precv, ssend, srecv, tsend, trecv, lsend, lrecv, zsend, zrecv,
     hsend, hrecv, gsend, grecv,
 ):
@@ -398,16 +399,16 @@
     targets = (other_time, above, below)
     lines = sites // LX
 
-    def first_z_copy(which, site):
+    def first_z_copy(half, which, site):
         return pltpu.make_async_remote_copy(
-            src_ref=first_round.at[site], dst_ref=first_z.at[which, site],
-            send_sem=zsend.at[0], recv_sem=zrecv.at[which],
+            src_ref=first_round.at[site, half], dst_ref=first_z.at[half, which, site],
+            send_sem=zsend.at[0], recv_sem=zrecv.at[half, which],
             device_id={"ta": targets[1 + which]}, device_id_type=MESH,
         )
 
-    def forward(site):
+    def forward(half, site):
         for which in range(2):
-            first_z_copy(which, site).start()
+            first_z_copy(half, which, site).start()
 
     weights_copy(partner, partner).wait_recv()
     sent, held = restricted(partner, weights_in), restricted(me, proj_ref)
@@ -420,9 +421,10 @@
     own_rounded = own.astype(jnp.bfloat16)
     hi_out[0] = own_rounded
     first_round[chip] = own_rounded
+    own_rest = coded(own - own_rounded.astype(jnp.float32))
     for half in range(2):
-        source_ref[half, chip] = own[half]
-    forward(chip)
+        lo_in[half, chip] = own_rest[half]
+    forward(0, chip)
 
     def arranged(at):
         group = at // 2
@@ -451,27 +453,17 @@
         def forward_step(at, carry):
             site = flipped(chip, arranged(at), bits - 1)
             source_copy(0, site).wait_recv()
-            forward(site)
+            forward(0, site)
             return carry
 
         lax.fori_loop(1, chips, forward_step, 0)
-
-    def complete_source(half):
-        def complete_step(step, carry):
-            site = flipped(chip, step, bits - 1)
-            high = first_round[site, half].astype(jnp.float32)
-            source_ref[half, site] = high + decoded(lo_in[half, site])
-            return carry
-
-        total_wait(lo_in.at[half, pl.ds(0, sites - 1)], lrecv.at[half])
-        lax.fori_loop(1, chips, complete_step, 0)
 
     mass = mass_ref[0]
 
     def place(site, dx, dy):
         return ((site // LX + dy) % lines) * LX + (site % LX + dx) % LX
 
-    pieces = 2
+    pieces = 4
     span = sites // pieces
 
     def z_copy(it, half, which):
@@ -501,7 +493,7 @@
         )
 
     def residual_at(it, half, site):
-        return source_ref[half, site] if it == 0 else res_half[half, site]
+        return source_ref[half, site] if it == 0 else res_half[it - 1, half, site]
 
     def rounded_at(it, half, site):
         return first_round[site, half] if it == 0 else round_ref[it - 1, half, site]
@@ -509,14 +501,7 @@
     def halo_at(it, half, which, site):
         if it > 0:
             return halo_ref[it - 1, half, which, site]
-        return first_t[half, site] if which == 0 else first_z[which - 1, site, half]
-
-    def send_halo(it, half):
-        for site in range(sites):
-            round_ref[it - 1, half, site] = res_half[half, site].astype(jnp.bfloat16)
-        pl.when(outer == 0)(lambda: send_t(it, half))
-        for which in range(1, 3):
-            z_copy(it, half, which).start()
+        return first_t[half, site] if which == 0 else first_z[half, which - 1, site]
 
     def send_late_halo(it, half):
         pl.when(outer == 1)(lambda: send_t(it, half))
@@ -529,7 +514,7 @@
             right = jnp.concatenate(
                 [wide_ref[half, place(site, dx, dy)] for dx, dy in steps], axis=0
             )
-            acc_ref[half, site] = jnp.dot(
+            acc_ref[it % 2, half, site] = jnp.dot(
                 near_ref[site], right, preferred_element_type=jnp.float32
             )
 
@@ -537,14 +522,14 @@
         right = jnp.concatenate(
             [widened(halo_at(it, half, 2, site)), widened(halo_at(it, half, 1, site))], axis=0
         )
-        return acc_ref[half, site] + jnp.dot(
+        return acc_ref[it % 2, half, site] + jnp.dot(
             zlinks_ref[site], right, preferred_element_type=jnp.float32
         )
 
     def t_product(it, half, site):
         wide = widened(halo_at(it, half, 0, site))
         right = jnp.concatenate([wide, wide], axis=0)
-        return acc_ref[half, site] + jnp.dot(
+        return acc_ref[it % 2, half, site] + jnp.dot(
             tlinks_ref[site], right, preferred_element_type=jnp.float32
         )
 
@@ -552,30 +537,34 @@
         return product + mass * rounded_at(it, half, site).astype(jnp.float32)
 
     def add_sums(it, half, site, q, sums):
-        r = residual_at(it, half, site)
-        q_other = swapped(q)
         sums[0] += q * q
-        sums[1] += q * r
-        sums[2] += q * swapped(r)
+        sums[1] += q * residual_at(it, half, site)
+        sums[2] += q * res_turned[half, site]
         for j in range(it):
-            b = basis_q[j, half, site]
-            sums[3 + 2 * j] += b * q
-            sums[4 + 2 * j] += b * q_other
+            sums[3 + 2 * j] += basis_q[j, half, site] * q
+            sums[4 + 2 * j] += turned_q[j, half, site] * q
 
     def first_t_product(half):
         total_wait(first_t.at[half, pl.ds(0, sites - 1)], trecv.at[half])
         for site in range(sites):
-            acc_ref[half, site] = t_product(0, half, site)
+            acc_ref[0, half, site] = t_product(0, half, site)
 
     def first_z_product(half):
-        if half == 0:
-            for which in range(2):
-                total_wait(first_z.at[which], zrecv.at[which])
+        for which in range(2):
+            total_wait(first_z.at[half, which], zrecv.at[half, which])
+        for site in range(sites):
+            product = z_product(0, half, site)
+            acc_ref[0, half, site] = full_product(0, half, site, product)
+
+    def first_stats(half):
+        total_wait(lo_in.at[half, pl.ds(0, sites - 1)], lrecv.at[half])
         sums = [0.0] * 3
         for site in range(sites):
-            q = full_product(0, half, site, z_product(0, half, site))
-            acc_ref[half, site] = q
-            add_sums(0, half, site, q, sums)
+            high = first_round[site, half].astype(jnp.float32)
+            whole = high + decoded(lo_in[half, site])
+            source_ref[half, site] = whole
+            res_turned[half, site] = turned(whole)
+            add_sums(0, half, site, acc_ref[0, half, site], sums)
         send_stats(0, half, sums)
 
     def far_product(it, half):
@@ -583,13 +572,13 @@
             z_copy(it, half, which).wait_recv()
         for site in range(sites):
             product = z_product(it, half, site)
-            acc_ref[half, site] = full_product(it, half, site, product)
+            acc_ref[it % 2, half, site] = full_product(it, half, site, product)
         sums = [0.0] * (3 + 2 * it)
         for site in range(sites):
             if site % span == 0:
                 t_copy(it, half, site // span).wait_recv()
             q = t_product(it, half, site)
-            acc_ref[half, site] = q
+            acc_ref[it % 2, half, site] = q
             add_sums(it, half, site, q, sums)
         send_stats(it, half, sums)
 
@@ -597,22 +586,20 @@
         lines_of = [jnp.sum(value, axis=0, keepdims=True) for value in sums]
         lines_of += [jnp.zeros((8 - len(lines_of), rhs), jnp.float32)]
         stats = jnp.concatenate(lines_of, axis=0)
-        moved = swapped(stats)
-        low = lower_lanes(stats.shape)
-        reals = stats + moved
-        imags = jnp.where(low, stats - moved, moved - stats)
+        stats = stats + swapped(stats)
+        low = lower_lanes((1, rhs))
+        rows = [stats[at : at + 1] for at in range(7)]
         packed = jnp.concatenate(
-            [reals[0:1]]
-            + [
-                jnp.where(low[0:1], reals[at : at + 1], imags[at + 1 : at + 2])
-                for at in (1, 3, 5)
-            ],
+            [rows[0], jnp.where(low, rows[1], -rows[2])]
+            + [jnp.where(low, rows[at], rows[at + 1]) for at in (3, 5)],
             axis=0,
         )
         stat_out[it, half] = packed
         for other in others[:0:-1]:
             stat_copy(it, half, other).start()
         stat_in[it, half, me] = packed
+        for site in range(sites):
+            acc_turned[half, site] = turned(acc_ref[it % 2, half, site])
 
     scalars = [([], [], [], []) for _ in range(2)]
 
@@ -646,27 +633,55 @@
             )
         backs.append((alpha[0] * epsilon, alpha[1] * epsilon))
         epsilons.append(epsilon)
+        gamma = (alpha[0] * factor, alpha[1] * factor)
+        betas = [
+            (gamma[0] * c_re - gamma[1] * c_im, gamma[0] * c_im + gamma[1] * c_re)
+            for c_re, c_im in coefs
+        ]
         for site in range(sites):
-            residual = residual_at(it, half, site)
-            q = acc_ref[half, site]
-            p = residual
-            for j in range(it):
-                q = q - times(coefs[j], basis_q[j, half, site])
-                p = p - times(coefs[j], basis_p[j, half, site])
-            q = q * factor
-            p = p * factor
+            change = gamma[0] * acc_ref[it % 2, half, site] + gamma[1] * acc_turned[half, site]
+            for j, beta in enumerate(betas):
+                change -= beta[0] * basis_q[j, half, site] + beta[1] * turned_q[j, half, site]
+            new_res = residual_at(it, half, site) - change
             if it < ITERS - 1:
-                basis_q[it, half, site] = q
-                basis_p[it, half, site] = p
-            step = times(alpha, p)
-            new_sol = step if it == 0 else sol_half[half, site] + step
-            new_res = residual - times(alpha, q)
-            if it < ITERS - 1 or half == 0:
-                sol_half[half, site] = new_sol
-                res_half[half, site] = new_res
+                res_half[it, half, site] = new_res
+                round_ref[it, half, site] = new_res.astype(jnp.bfloat16)
+                if site % span == span - 1:
+                    pl.when(outer == 0)(lambda: t_copy(it + 1, half, site // span).start())
+            elif half == 0:
+                res_half[it, half, site] = new_res
             else:
-                unpack(sol_ref, site, sol_half[0, site], new_sol)
-                unpack(res_ref, site, res_half[0, site], new_res)
+                unpack(res_ref, site, res_half[it, 0, site], new_res)
+        if it < ITERS - 1:
+            for which in range(1, 3):
+                z_copy(it + 1, half, which).start()
+
+        def remaining():
+            for site in range(sites):
+                residual = residual_at(it, half, site)
+                step = gamma[0] * residual + gamma[1] * res_turned[half, site]
+                for j, beta in enumerate(betas):
+                    step -= beta[0] * basis_p[j, half, site] + beta[1] * turned_p[j, half, site]
+                new_sol = step if it == 0 else sol_half[half, site] + step
+                if it == ITERS - 1 and half == 1:
+                    unpack(sol_ref, site, sol_half[0, site], new_sol)
+                else:
+                    sol_half[half, site] = new_sol
+                if it < ITERS - 1:
+                    q = acc_ref[it % 2, half, site]
+                    p = residual
+                    for j, (c_re, c_im) in enumerate(coefs):
+                        q -= c_re * basis_q[j, half, site] + c_im * turned_q[j, half, site]
+                        p -= c_re * basis_p[j, half, site] + c_im * turned_p[j, half, site]
+                    q = q * factor
+                    p = p * factor
+                    basis_q[it, half, site] = q
+                    basis_p[it, half, site] = p
+                    turned_q[it, half, site] = turned(q)
+                    turned_p[it, half, site] = turned(p)
+                    res_turned[half, site] = turned(res_half[it, half, site])
+
+        return remaining
 
     def unpack(to_ref, site, first, second):
         low = lower_lanes(first.shape)
@@ -680,23 +695,27 @@
     near_product(0, 0)
     near_product(0, 1)
     first_t_product(0)
+    for site in range(sites):
+        forward(1, site)
     send_after(1)
     send_rest(1)
-    complete_source(0)
     first_z_product(0)
+    first_stats(0)
     first_t_product(1)
-    complete_source(1)
     first_z_product(1)
+    first_stats(1)
     for it in range(ITERS):
         if it > 0:
             for half in range(2):
                 far_product(it, half)
         for half in range(2):
-            update(it, half)
+            remaining = update(it, half)
             if it < ITERS - 1:
-                send_halo(it + 1, half)
                 near_product(it + 1, half)
+            remaining()
+            if it < ITERS - 1:
                 send_late_halo(it + 1, half)
+
     total_wait(proj_ref.at[pl.ds(0, count - 1)], wsend.at[0])
     total_wait(part_out, psend.at[0])
     total_wait(hi_out.at[pl.ds(0, chips - 1)], ssend.at[0])
@@ -770,14 +789,18 @@
             pltpu.VMEM((2, sites, comps, rhs), bf16),
             pltpu.VMEM((2, sites, comps, rhs), f32),
             pltpu.VMEM((sites, 2, comps, rhs), bf16),
-            pltpu.VMEM((2, sites, 2, comps, rhs), bf16),
+            pltpu.VMEM((2, 2, sites, comps, rhs), bf16),
             pltpu.VMEM((2, sites, comps, rhs), bf16),
             pltpu.VMEM((2, sites, 2 * comps, rhs), bf16),
             pltpu.VMEM((ITERS - 1, 2, *half), bf16),
             pltpu.VMEM((ITERS - 1, 2, 3, *half), bf16),
+            pltpu.VMEM((2, 2, *half), f32),
             pltpu.VMEM((2, *half), f32),
             pltpu.VMEM((2, *half), f32),
+            pltpu.VMEM((ITERS, 2, *half), f32),
             pltpu.VMEM((2, *half), f32),
+            pltpu.VMEM((ITERS - 1, 2, *half), f32),
+            pltpu.VMEM((ITERS - 1, 2, *half), f32),
             pltpu.VMEM((ITERS - 1, 2, *half), f32),
             pltpu.VMEM((ITERS - 1, 2, *half), f32),
             pltpu.VMEM((ITERS, 2, 4, rhs), f32),
@@ -794,9 +817,9 @@
             dma((1,)),
             dma((2,)),
             dma((1,)),
-            dma((2,)),
+            dma((2, 2)),
             dma((1,)),
-            dma((2, 4)),
+            dma((2, 6)),
             dma((1,)),
             dma((ITERS, 2)),
         ],

time: 68.9 us -> 67.1 us (0.974)
  Pallas kernels: 67.5 us -> 65.6 us
    pallas_call x1, Pallas kernels: 66.6 us -> 64.7 us  [shards_kernel(): pl.pallas_call(functools.partial(solve_kernel, count, sites, comps), out_...]
where the time goes in v4:
time: 67.1 us; the launch traced here: 66.9 us
  Pallas kernels  65.6 us (98%)
  between operations  1.29 us (2%)
    pallas_call x1, Pallas kernels, shards_kernel(): pl.pallas_call(functools.partial(solve_kernel, count, sites, comps), out_...  64.7 us

profile of v4, /device:TPU:0, one launch (start us, length us, event | category | flops | bytes accessed | tf_op | source)
XLA Modules:
  0.0 66.9 jit_solution(15633857829968163381)
XLA Ops:
  1.3 64.7 %shard_map.59 = (f32[8,96,128]{2,1,0:T(8,128)S(1)}, f32[8,96,128]{2,1,0:T(8,128)S(1)}) custom-call(f32[1]{0:T(128)S(6)} %copy.6.mass_ref, bf16[16,8,2304]{2,1,0:T(8,128)(2,1)} %bitcast.7, bf16[16,768,128]{2,1,0:T(8,128)(2,1)} %bitcast.5, bf16[8,48,864]{2,1,0:T(8,128)(2,1)} %bitcast.6), custom_call_target="tpu_custom_call" | custom-call | tf_op jit(solution)/shard_map/pallas_call | solution.py:770
  66.0 0.9 %shard_map.60 = (f32[8,96,128]{2,1,0:T(8,128)}, f32[8,96,128]{2,1,0:T(8,128)}) custom-call(f32[8,96,128]{2,1,0:T(8,128)S(1)} %get-tuple-element.6.sol_ref, f32[8,96,128]{2,1,0:T(8,128)S(1)} %get-tuple-element.7.res_ref), custom_call_target="tpu_custom_call" | custom-call | tf_op jit(solution)/shard_map/pallas_call | solution.py:743

commit v5 on v4

--- a/solution.py
+++ b/solution.py
@@ -286,7 +286,7 @@
     def weights_copy(other, origin):
         return pltpu.make_async_remote_copy(
             src_ref=proj_ref.at[other], dst_ref=weights_in.at[origin],
-            send_sem=wsend.at[0], recv_sem=wrecv.at[origin],
+            send_sem=wsend.at[0], recv_sem=wrecv.at[origin // 2],
             device_id={"ta": other}, device_id_type=MESH,
         )
 
@@ -376,8 +376,7 @@
         other = flipped(chip, step, bits - 1)
         away = other * 2 + 1 - core
         kept = other * 2 + core
-        weights_copy(partner, away).wait_recv()
-        weights_copy(partner, kept).wait_recv()
+        total_wait(weights_in.at[pl.ds(other * 2, 2)], wrecv.at[other])
         sent, held = restricted(away, weights_in), restricted(kept, weights_in)
         part_out[step] = sent
         part_keep[step] = held
@@ -463,7 +462,7 @@
     def place(site, dx, dy):
         return ((site // LX + dy) % lines) * LX + (site % LX + dx) % LX
 
-    pieces = 4
+    pieces = 2
     span = sites // pieces
 
     def z_copy(it, half, which):
@@ -694,10 +693,10 @@
     pl.when(outer == 1)(lambda: send_rest(0))
     near_product(0, 0)
     near_product(0, 1)
-    first_t_product(0)
     for site in range(sites):
         forward(1, site)
     send_after(1)
+    first_t_product(0)
     send_rest(1)
     first_z_product(0)
     first_stats(0)
@@ -807,7 +806,7 @@
             pltpu.VMEM((ITERS, 2, count, 4, rhs), f32),
             dma((3,)),
             dma((1,)),
-            dma((count,)),
+            dma((chips,)),
             dma((1,)),
             dma((chips,)),
             dma((1,)),
@@ -819,7 +818,7 @@
             dma((1,)),
             dma((2, 2)),
             dma((1,)),
-            dma((2, 6)),
+            dma((2, 4)),
             dma((1,)),
             dma((ITERS, 2)),
         ],

time: 67.1 us -> 66.9 us (level)
  no operation moved by 1% of the time
where the time goes in v5:
time: 66.9 us; the launch traced here: 66.8 us
  Pallas kernels  65.5 us (98%)
  between operations  1.29 us (2%)
    pallas_call x1, Pallas kernels, shards_kernel(): pl.pallas_call(functools.partial(solve_kernel, count, sites, comps), out_...  64.6 us

profile of v5, /device:TPU:0, one launch (start us, length us, event | category | flops | bytes accessed | tf_op | source)
XLA Modules:
  0.0 66.8 jit_solution(864642817708410956)
XLA Ops:
  1.3 64.6 %shard_map.59 = (f32[8,96,128]{2,1,0:T(8,128)S(1)}, f32[8,96,128]{2,1,0:T(8,128)S(1)}) custom-call(f32[1]{0:T(128)S(6)} %copy.6.mass_ref, bf16[16,8,2304]{2,1,0:T(8,128)(2,1)} %bitcast.7, bf16[16,768,128]{2,1,0:T(8,128)(2,1)} %bitcast.5, bf16[8,48,864]{2,1,0:T(8,128)(2,1)} %bitcast.6), custom_call_target="tpu_custom_call" | custom-call | tf_op jit(solution)/shard_map/pallas_call | solution.py:769
  65.9 0.9 %shard_map.60 = (f32[8,96,128]{2,1,0:T(8,128)}, f32[8,96,128]{2,1,0:T(8,128)}) custom-call(f32[8,96,128]{2,1,0:T(8,128)S(1)} %get-tuple-element.6.sol_ref, f32[8,96,128]{2,1,0:T(8,128)S(1)} %get-tuple-element.7.res_ref), custom_call_target="tpu_custom_call" | custom-call | tf_op jit(solution)/shard_map/pallas_call | solution.py:742

commit v6 on v5

--- a/solution.py
+++ b/solution.py
@@ -237,7 +237,10 @@
 
 def decoded(code):
     value = code.astype(jnp.float32)
-    root = jnp.sqrt(jnp.sqrt(jnp.sqrt(jnp.abs(value)))) * (1.0 / CODE_SCALE)
+    size = jnp.abs(value)
+    fourth = lax.rsqrt(lax.rsqrt(size))
+    root = fourth * lax.rsqrt(fourth) * (1.0 / CODE_SCALE)
+    root = jnp.where(size >= 2.0**-126, root, 0.0)
     return jnp.where(value < 0.0, -root, root)
 
 

time: 66.9 us -> 66.8 us (level)
  no operation moved by 1% of the time
where the time goes in v6:
time: 66.8 us; the launch traced here: 66.7 us
  Pallas kernels  65.4 us (98%)
  between operations  1.29 us (2%)
    pallas_call x1, Pallas kernels, shards_kernel(): pl.pallas_call(functools.partial(solve_kernel, count, sites, comps), out_...  64.5 us

profile of v6, /device:TPU:0, one launch (start us, length us, event | category | flops | bytes accessed | tf_op | source)
XLA Modules:
  0.0 66.7 jit_solution(5701957158098863835)
XLA Ops:
  1.3 64.5 %shard_map.59 = (f32[8,96,128]{2,1,0:T(8,128)S(1)}, f32[8,96,128]{2,1,0:T(8,128)S(1)}) custom-call(f32[1]{0:T(128)S(6)} %copy.6.mass_ref, bf16[16,8,2304]{2,1,0:T(8,128)(2,1)} %bitcast.7, bf16[16,768,128]{2,1,0:T(8,128)(2,1)} %bitcast.5, bf16[8,48,864]{2,1,0:T(8,128)(2,1)} %bitcast.6), custom_call_target="tpu_custom_call" | custom-call | tf_op jit(solution)/shard_map/pallas_call | solution.py:772
  65.8 0.9 %shard_map.60 = (f32[8,96,128]{2,1,0:T(8,128)}, f32[8,96,128]{2,1,0:T(8,128)}) custom-call(f32[8,96,128]{2,1,0:T(8,128)S(1)} %get-tuple-element.6.sol_ref, f32[8,96,128]{2,1,0:T(8,128)S(1)} %get-tuple-element.7.res_ref), custom_call_target="tpu_custom_call" | custom-call | tf_op jit(solution)/shard_map/pallas_call | solution.py:745
